TPU v7x, 16 devices: a whole 2x2x2 slice. The times are simulated.
16 devices in a mesh: stage: 2 (over z), expert: 8 (over y, x, core).
Axes of the slice: x: 2, y: 2, z: 2, core: 2. Of those that a mesh axis runs over, the one named last changes fastest.
Arguments:
- w_gate: bfloat16 [2, 8, 2048, 1024], P('stage', 'expert')
- w_up: bfloat16 [2, 8, 2048, 1024], P('stage', 'expert')
- w_down: bfloat16 [2, 8, 1024, 2048], P('stage', 'expert')
- hot_units: int32 [1], replicated
- slot_map: int32 [16, 2], replicated
Outputs:
- output 1: bfloat16 [2, 48, 2048, 1024], P(None, ('stage', 'expert'))
- output 2: bfloat16 [2, 48, 512, 2048], P(None, ('stage', 'expert'))
All inputs are finite; a program needn't handle non-finite values.
Results may differ from a plain program's by a relative error of at most 0.001.
Values are sent between devices in bfloat16 or wider.
A program may use at most 1 GiB of HBM per device.

v0:
```python
import jax
import jax.numpy as jnp
from jax import lax
from jax.sharding import PartitionSpec as P


def solution(mesh):
    stage_count = mesh.shape['stage']
    group_count = mesh.shape['expert']
    devices_flat = stage_count * group_count
    flat_axes = ('stage', 'expert')
    perm_pairs = [(stage_idx * group_count + rank_idx, rank_idx * stage_count + stage_idx) for stage_idx in range(stage_count) for rank_idx in range(group_count)]

    def local_handover(gate_blk, up_blk, down_blk, hot_units, slot_map):
        layers_stage, experts_rank, d_model, ff_expert = gate_blk.shape
        layers = layers_stage * stage_count
        experts = experts_rank * group_count
        split_count = max(devices_flat // experts, 1)
        units_dev = max(experts // devices_flat, 1)
        ff_dev = ff_expert // split_count
        gate_parts = gate_blk.reshape(layers_stage, experts_rank, d_model, split_count, ff_dev)
        up_parts = up_blk.reshape(layers_stage, experts_rank, d_model, split_count, ff_dev)
        fused_send = jnp.concatenate([gate_parts, up_parts], axis=-1).transpose(0, 1, 3, 2, 4).reshape(layers_stage, stage_count, units_dev, d_model, 2 * ff_dev)
        down_send = down_blk.reshape(layers_stage, stage_count, units_dev, ff_dev, d_model)
        fused_recv = lax.all_to_all(fused_send, 'stage', 1, 0, tiled=True).reshape(layers, units_dev, d_model, 2 * ff_dev)
        down_recv = lax.all_to_all(down_send, 'stage', 1, 0, tiled=True).reshape(layers, units_dev, ff_dev, d_model)
        fused_home = lax.ppermute(fused_recv, flat_axes, perm_pairs)
        down_home = lax.ppermute(down_recv, flat_axes, perm_pairs)
        my_flat = lax.axis_index('stage') * group_count + lax.axis_index('expert')
        owned_mask = (hot_units // units_dev == my_flat)[None, :, None, None]
        local_pick = hot_units % units_dev
        fused_hot = lax.psum(jnp.where(owned_mask, jnp.take(fused_home, local_pick, axis=1), 0), flat_axes)
        down_hot = lax.psum(jnp.where(owned_mask, jnp.take(down_home, local_pick, axis=1), 0), flat_axes)
        my_slots = lax.dynamic_index_in_dim(slot_map, my_flat, axis=0, keepdims=False)
        slot_used = (my_slots >= 0)[None, :, None, None]
        hot_pick = jnp.maximum(my_slots, 0)
        fused_extra = jnp.where(slot_used, jnp.take(fused_hot, hot_pick, axis=1), 0)
        down_extra = jnp.where(slot_used, jnp.take(down_hot, hot_pick, axis=1), 0)
        return jnp.concatenate([fused_home, fused_extra], axis=1), jnp.concatenate([down_home, down_extra], axis=1)

    return jax.shard_map(local_handover, mesh=mesh, in_specs=(P('stage', 'expert'), P('stage', 'expert'), P('stage', 'expert'), P(), P()), out_specs=(P(None, flat_axes), P(None, flat_axes)), check_vma=False)
```

profile of v0, /device:TPU:0, one launch (start us, length us, event | category | flops | bytes accessed | tf_op | source)
XLA Modules:
  0.0 540.9 jit_solution(11264058621434610737)
XLA Ops:
  7.2 0.0 all-reduce.3.cloned.1.call-start
  7.2 6.5 %copy.11 = bf16[1,1,2048,1024]{2,3,1,0:T(8,128)(2,1)} copy(bf16[1,1,2048,1024]{3,2,1,0:T(8,128)(2,1)} %param.5) | data formatting | bytes 8388608 | tf_op args[0]
  13.7 6.4 %copy.12 = bf16[1,1,2048,1024]{2,3,1,0:T(8,128)(2,1)} copy(bf16[1,1,2048,1024]{3,2,1,0:T(8,128)(2,1)} %param.6) | data formatting | bytes 8388608 | tf_op args[1]
  20.1 8.5 %maximum_bitcast_fusion = bf16[1,2,1,2048,1024]{3,4,2,0,1:T(8,128)(2,1)} fusion(bf16[1,1,2048,2,512]{2,4,3,1,0:T(8,128)(2,1)} %bitcast.17, bf16[1,1,2048,2,512]{2,4,3,1,0:T(8,128)(2,1)} %bitcast.16), kind=kLoop, calls=%fused_computation.3 | loop fusion | flops 16777216 | bytes 16777216 | tf_op jit(solution)/shard_map/reshape | solution.py:23
  28.6 105.2 %all_to_all.8 = bf16[1,2,1,2048,1024]{3,4,2,0,1:T(8,128)(2,1)} all-to-all(bf16[1,2,1,2048,1024]{3,4,2,0,1:T(8,128)(2,1)} %maximum_bitcast_fusion), channel_id=1, replica_groups=mesh['stage'=2,'expert'=8] {'stage'}, dimensions={1} | all-to-all | bytes 16777216 | tf_op jit(solution)/shard_map/all_to_all | solution.py:25
  133.8 64.0 %collective-permute-start = (bf16[2,1,2048,1024]{2,3,0,1:T(8,128)(2,1)}, bf16[2,1,2048,1024]{2,3,0,1:T(8,128)(2,1)}, u32[]{:S(2)}, u32[]{:S(2)}) collective-permute-start(bf16[2,1,2048,1024]{2,3,0,1:T(8,128)(2,1)} %bitcast.5), channel_id=1, source_target_pairs={{0,0},{1,2},{2,4},{3,6},{4,8},{5,10},{6,12},{7,14},{8,1},{9,3},{10... | collective-permute-start | bytes 25165832 | tf_op jit(solution)/shard_map/ppermute | solution.py:27
  197.8 0.0 copy-done.2
  197.8 75.2 %all_to_all.9 = bf16[1,2,1,512,2048]{4,3,2,0,1:T(8,128)(2,1)} all-to-all(bf16[1,2,1,512,2048]{4,3,2,0,1:T(8,128)(2,1)S(1)} %bitcast.20), channel_id=1, replica_groups=mesh['stage'=2,'expert'=8] {'stage'}, dimensions={1} | all-to-all | bytes 8388608 | tf_op jit(solution)/shard_map/all_to_all | solution.py:26
  273.1 32.8 %collective-permute-start.1 = (bf16[2,1,512,2048]{3,2,0,1:T(8,128)(2,1)}, bf16[2,1,512,2048]{3,2,0,1:T(8,128)(2,1)}, u32[]{:S(2)}, u32[]{:S(2)}) collective-permute-start(bf16[2,1,512,2048]{3,2,0,1:T(8,128)(2,1)} %bitcast.10), channel_id=1, source_target_pairs={{0,0},{1,2},{2,4},{3,6},{4,8},{5,10},{6,12},{7,14},{8,1},{9,3},{10... | collective-permute-start | bytes 12582920 | tf_op jit(solution)/shard_map/ppermute | solution.py:28
  306.6 0.0 collective-permute-done.1
  306.6 2.3 broadcast_select_fusion.1
  308.9 0.0 collective-permute-done
  308.9 3.9 broadcast_select_fusion
  312.8 0.0 all-reduce.3.cloned.1.call-update
  312.9 0.7 copy-done.3
  313.5 0.2 compare_reduce_fusion.1
  313.7 11.9 %copy.15 = bf16[2,1,2048,1024]{3,2,1,0:T(8,128)(2,1)} copy(bf16[2,1,2048,1024]{2,3,0,1:T(8,128)(2,1)} %collective-permute-done) | data formatting | bytes 16777216 | tf_op jit(solution)/shard_map/ppermute | solution.py:27
  325.6 151.6 %all-reduce.3.cloned.1.call-done = (bf16[2,1,2048,1024]{2,3,0,1:T(8,128)(2,1)}, bf16[2,1,512,2048]{3,2,0,1:T(8,128)(2,1)}) async-done(((bf16[2,1,2048,1024]{2,3,0,1:T(8,128)(2,1)}, bf16[2,1,512,2048]{3,2,0,1:T(8,128)(2,1)}), (bf16[2,1,2048,1024]{2,3,0,1:T(8,128)(2,1)}, bf16[2,1,512,2048]{3,2,0,1:T(8,128)(2,1)})) %all-reduce.3.cloned.1.call-update) | async-done | bytes 12582928 | tf_op jit(solution)/shard_map/psum | solution.py:32
  477.2 11.8 %copy.14 = bf16[2,2048,1024]{2,1,0:T(8,128)(2,1)} copy(bf16[2,2048,1024]{1,2,0:T(8,128)(2,1)} %bitcast.18) | data formatting | bytes 16777216 | tf_op jit(solution)/shard_map/jit(_take)/gather | solution.py:37
  489.1 11.8 %select_select_fusion = bf16[2,2,2048,1024]{3,2,1,0:T(8,128)(2,1)} fusion(pred[2]{0:T(512)(128)(4,1)S(1)} %get-tuple-element.3, pred[2]{0:T(512)(128)(4,1)S(1)} %get-tuple-element.2, bf16[2,2048,1024]{2,1,0:T(8,128)(2,1)} %copy.14), kind=kLoop, calls=%fused_computation.1 | loop fusion | flops 16777216 | bytes 25165828 | tf_op jit(solution)/shard_map/jit(_where)/select_n | solution.py:37
  500.8 0.0 copy-done.1
  500.8 4.4 select_select_fusion.1
  505.2 21.1 %pad_maximum_fusion = bf16[2,3,2048,1024]{3,2,1,0:T(8,128)(2,1)} fusion(bf16[2,2,2048,1024]{3,2,1,0:T(8,128)(2,1)} %select_select_fusion, bf16[2,1,2048,1024]{3,2,1,0:T(8,128)(2,1)} %copy.15), kind=kLoop, calls=%fused_computation | loop fusion | flops 12582912 | bytes 50331648 | tf_op jit(solution)/shard_map/concatenate | solution.py:39
  526.4 7.7 %pad_maximum_fusion.1 = bf16[2,3,512,2048]{3,2,1,0:T(8,128)(2,1)} fusion(bf16[2,2,512,2048]{3,2,1,0:T(8,128)(2,1)S(1)} %copy-done, bf16[2,1,512,2048]{3,2,1,0:T(8,128)(2,1)} %bitcast.11), kind=kLoop, calls=%fused_computation.2 | loop fusion | flops 6291456 | bytes 25165824 | tf_op jit(solution)/shard_map/concatenate | solution.py:39
  (5 shorter events, 0.0 us)
Async XLA Ops:
  7.2 470.1 %all-reduce.3.cloned.1.call-start = ((), (), s32[]{:S(2)}) async-start(), calls=%async_computation.2 | async-start | bytes 25165824 | tf_op jit(solution)/shard_map/psum | solution.py:32
  28.6 169.2 %copy-start.2 = (bf16[1,1,1024,2048]{3,2,1,0:T(8,128)(2,1)S(1)}, bf16[1,1,1024,2048]{3,2,1,0:T(8,128)(2,1)}, u32[]{:S(2)}) copy-start(bf16[1,1,1024,2048]{3,2,1,0:T(8,128)(2,1)} %param.7) | copy-start | bytes 12582916
  133.8 175.1 %collective-permute-start = (bf16[2,1,2048,1024]{2,3,0,1:T(8,128)(2,1)}, bf16[2,1,2048,1024]{2,3,0,1:T(8,128)(2,1)}, u32[]{:S(2)}, u32[]{:S(2)}) collective-permute-start(bf16[2,1,2048,1024]{2,3,0,1:T(8,128)(2,1)} %bitcast.5), channel_id=1, source_target_pairs={{0,0},{1,2},{2,4},{3,6},{4,8},{5,10},{6,12},{7,14},{8,1},{9,3},{10... | collective-permute-start | bytes 25165832 | tf_op jit(solution)/shard_map/ppermute | solution.py:27
  273.1 33.5 %collective-permute-start.1 = (bf16[2,1,512,2048]{3,2,0,1:T(8,128)(2,1)}, bf16[2,1,512,2048]{3,2,0,1:T(8,128)(2,1)}, u32[]{:S(2)}, u32[]{:S(2)}) collective-permute-start(bf16[2,1,512,2048]{3,2,0,1:T(8,128)(2,1)} %bitcast.10), channel_id=1, source_target_pairs={{0,0},{1,2},{2,4},{3,6},{4,8},{5,10},{6,12},{7,14},{8,1},{9,3},{10... | collective-permute-start | bytes 12582920 | tf_op jit(solution)/shard_map/ppermute | solution.py:28
  312.8 0.7 copy-start.3
  489.0 11.8 %copy-start.1 = (bf16[2,1,512,2048]{3,2,0,1:T(8,128)(2,1)S(1)}, bf16[2,1,512,2048]{3,2,0,1:T(8,128)(2,1)}, u32[]{:S(2)}) copy-start(bf16[2,1,512,2048]{3,2,0,1:T(8,128)(2,1)} %get-tuple-element.5) | copy-start | bytes 12582916
  505.2 21.2 %copy-start = (bf16[2,2,512,2048]{3,2,1,0:T(8,128)(2,1)S(1)}, bf16[2,2,512,2048]{3,2,1,0:T(8,128)(2,1)}, u32[]{:S(2)}) copy-start(bf16[2,2,512,2048]{3,2,1,0:T(8,128)(2,1)} %select_select_fusion.1) | copy-start | bytes 25165828
Sparse Core Ops, SparseCore 0:
  313.0 164.1 all-reduce.2
where the time goes:
time: 552 us; the launch traced here: 541 us
  blocking collectives  180 us (33%)
  waiting for transfers between devices  152 us (28%)
  starting transfers between devices  96.9 us (18%)
  other arithmetic  60 us (11%)
  local copies, waits for them, and re-layouts  37.3 us (7%)
  between operations  14.7 us (3%)
    psum x1, waiting for transfers between devices, local_handover(): lax.psum(jnp.where(owned_mask, jnp.take(fused_home, local_pick, axis=1),...  152 us
    all_to_all x1, blocking collectives, local_handover(): lax.all_to_all(fused_send, 'stage', 1, 0, tiled=True)  105 us
    all_to_all x1, blocking collectives, local_handover(): lax.all_to_all(down_send, 'stage', 1, 0, tiled=True)  75.2 us
    ppermute x1, starting transfers between devices, local_handover(): fused_home = lax.ppermute(fused_recv, flat_axes, perm_pairs)  64 us
    ppermute x1, starting transfers between devices, local_handover(): down_home = lax.ppermute(down_recv, flat_axes, perm_pairs)  32.8 us
    concatenate x1, other arithmetic, local_handover(): jnp.concatenate([fused_home, fused_extra], axis=1)  21.1 us
    unnamed x10, local copies, waits for them, and re-layouts  13.6 us
    ppermute x1, local copies, waits for them, and re-layouts, local_handover(): fused_home = lax.ppermute(fused_recv, flat_axes, perm_pairs)  11.9 us
  transfers between devices with their start and end apart: 3, of which 1 were waited for; matrix products, arithmetic and copies ran while one was open for 3% of the time, Pallas kernels for 0%

commit v1 on v0

v1 whole, which is shorter than its diff:
```python
import functools

import jax
import jax.numpy as jnp
from jax import lax
from jax.experimental import pallas as pl
from jax.experimental.pallas import tpu as pltpu
from jax.sharding import PartitionSpec as P

MESH = pl.DeviceIdType.MESH
ANY = pl.BlockSpec(memory_space=pl.ANY)
BF16 = jnp.bfloat16

PARENT = (
    (None, 0, 3, 1, 5, 1, 7, 5),
    (None, 3, 0, 2, 6, 7, 2, 3),
    (None, 5, 6, 7, 0, 4, 4, 6),
)
DEPTH = (
    (0, 1, 3, 2, 3, 2, 4, 3),
    (0, 3, 1, 2, 3, 4, 2, 3),
    (0, 3, 3, 4, 1, 2, 2, 3),
)
CHILDREN = tuple(tuple(tuple(v for v in range(1, 8) if par[v] == r) for r in range(8)) for par in PARENT)
N = 16


def coords():
    z = lax.axis_index("stage")
    j = lax.axis_index("expert")
    return z, j // 4, (j // 2) % 2, j % 2


def dev(z, y, x, q):
    return (z, y * 4 + x * 2 + q)


def flip(v, bit):
    return 1 - v if bit else v


def table(index, values):
    out = jnp.int32(values[0])
    for i, v in enumerate(values[1:], 1):
        if v != values[0]:
            out = jnp.where(index == i, jnp.int32(v), out)
    return out


def home_kernel(gate, up, down, home13, homed, vg, vd, load_sem, send_sem, recv_sem):
    s, a, b, c = coords()

    def source(k, p):
        if p == 2:
            return down.at[0, 0, pl.ds(k * 512, 512), :], vd.at[k]
        return (gate, up)[p].at[0, 0, :, pl.ds(k * 512, 512)], vg.at[k, p]

    def dest(layer, p):
        return homed.at[layer] if p == 2 else home13.at[layer, :, pl.ds(p * 512, 512)]

    loads = {}
    for p in range(3):
        for k in range(2):
            loads[k, p] = pltpu.make_async_copy(*source(k, p), load_sem.at[k, p])
            loads[k, p].start()
    stay = [(s == a) & (a == b) & (b == c) & (c == k) for k in range(2)]

    def send(k, p):
        return pltpu.make_async_remote_copy(
            src_ref=source(k, p)[1],
            dst_ref=dest(s, p),
            send_sem=send_sem.at[k, p],
            recv_sem=recv_sem.at[s, p],
            device_id=dev(a, b, c, k),
            device_id_type=MESH,
        )

    for p in range(3):
        for k in range(2):
            loads[k, p].wait()

            @pl.when(stay[k])
            def _():
                pltpu.make_async_copy(source(k, p)[1], dest(s, p), recv_sem.at[s, p]).start()

            @pl.when(jnp.logical_not(stay[k]))
            def _():
                send(k, p).start()

    for p in range(3):
        for k in range(2):

            @pl.when(jnp.logical_not(stay[k]))
            def _():
                send(k, p).wait_send()

    for layer in range(2):
        for p in range(3):
            pltpu.make_async_copy(dest(layer, p), dest(layer, p), recv_sem.at[layer, p]).wait()


def hot_kernel(unit, gate, up, down, hot13, hotd, vg, vd, load_sem, recv_sem, send_sem, side_send, side_recv, out_sem):
    e, k = unit // 2, unit % 2
    ra, rb, rc = e // 4, (e // 2) % 2, e % 2
    z, y, x, q = coords()

    def source(p):
        return down.at[0, 0, pl.ds(k * 512, 512), :] if p == 2 else (gate, up)[p].at[0, 0, :, pl.ds(k * 512, 512)]

    def held(s, p, i=None):
        if p == 2:
            return vd.at[s] if i is None else vd.at[s, pl.ds(i * (512 // N), 512 // N), :]
        return vg.at[s, p] if i is None else vg.at[s, p, pl.ds(i * (2048 // N), 2048 // N), :]

    def final(s, p, i=None):
        if p == 2:
            return hotd.at[s] if i is None else hotd.at[s, pl.ds(i * (512 // N), 512 // N), :]
        cols = pl.ds(p * 512, 512)
        return hot13.at[s, :, cols] if i is None else hot13.at[s, pl.ds(i * (2048 // N), 2048 // N), cols]

    state = []
    for s in range(2):
        fz, fy, fx = flip(z, s), flip(y, ra), flip(x, rb)
        rel = fz * 4 + fy * 2 + fx
        relay = q == jnp.where(rel == 0, rc, s)
        state.append((rel, relay, fz, fy, fx))

    for s in range(2):
        rel, relay = state[s][:2]

        @pl.when(relay & (rel == 0))
        def _():
            for p in range(3):
                pltpu.make_async_copy(source(p), held(s, p), load_sem.at[p]).start()
            for p in range(3):
                pltpu.make_async_copy(source(p), held(s, p), load_sem.at[p]).wait()

    def step(t, carry):
        for s in range(2):
            rel, relay, fz, fy, fx = state[s]
            for p in range(3):
                i = t - table(rel, DEPTH[p])

                @pl.when(relay & (i >= 0) & (i < N))
                def _():
                    @pl.when(rel != 0)
                    def _():
                        pltpu.make_async_copy(held(s, p, i), held(s, p, i), recv_sem.at[s, p, i]).wait()

                    for m in range(2):
                        nodes = [r for r in range(8) if len(CHILDREN[p][r]) > m]
                        if not nodes:
                            continue
                        child = table(rel, [CHILDREN[p][r][m] if r in nodes else -1 for r in range(8)])

                        @pl.when(child >= 0)
                        def _():
                            to = dev(flip(child // 4, s), flip((child // 2) % 2, ra), flip(child % 2, rb), s)
                            pltpu.make_async_remote_copy(
                                src_ref=held(s, p, i),
                                dst_ref=held(s, p, i),
                                send_sem=send_sem.at[s, p, m],
                                recv_sem=recv_sem.at[s, p, i],
                                device_id=to,
                                device_id_type=MESH,
                            ).start()

                    pltpu.make_async_remote_copy(
                        src_ref=held(s, p, i),
                        dst_ref=final(s, p, i),
                        send_sem=side_send.at[s, p],
                        recv_sem=side_recv.at[s, p],
                        device_id=dev(z, y, x, 1 - q),
                        device_id_type=MESH,
                    ).start()
                    pltpu.make_async_copy(held(s, p, i), final(s, p, i), out_sem.at[s, p]).start()

        return carry

    lax.fori_loop(0, N + max(map(max, DEPTH)), step, 0)

    for s in range(2):
        rel, relay = state[s][:2]
        for p in range(3):

            @pl.when(relay)
            def _():
                for m in range(2):
                    nodes = [r for r in range(8) if len(CHILDREN[p][r]) > m]
                    if not nodes:
                        continue

                    @pl.when(table(rel, [1 if r in nodes else 0 for r in range(8)]) == 1)
                    def _():
                        pltpu.make_async_copy(held(s, p), held(s, p), send_sem.at[s, p, m]).wait()

                pltpu.make_async_copy(held(s, p), held(s, p), side_send.at[s, p]).wait()
                pltpu.make_async_copy(held(s, p), final(s, p), out_sem.at[s, p]).wait()

            @pl.when(jnp.logical_not(relay))
            def _():
                pltpu.make_async_copy(final(s, p), final(s, p), side_recv.at[s, p]).wait()


def place_kernel(slots, home13, homed, hot13, hotd, out13, outd, va, vb, zero, in_sem, out_sem):
    me = lax.axis_index("stage") * 8 + lax.axis_index("expert")
    vah, vaH = va
    vbh, vbH = vb
    zero[...] = jnp.zeros_like(zero)
    pairs = []
    for g in range(4):
        layer, r = g // 2, g % 2
        rows = pl.ds(r * 1024, 1024)
        pairs.append((home13.at[layer, rows], vah.at[layer, rows], lambda t, layer=layer, rows=rows: out13.at[layer, t, rows], False, 0))
        pairs.append((hot13.at[layer, rows], vaH.at[layer, rows], lambda t, layer=layer, rows=rows: out13.at[layer, t, rows], True, 0))
    for layer in range(2):
        pairs.append((homed.at[layer], vbh.at[layer], lambda t, layer=layer: outd.at[layer, t], False, 1))
        pairs.append((hotd.at[layer], vbH.at[layer], lambda t, layer=layer: outd.at[layer, t], True, 1))
    for n, (src, mid, out, hot, kind) in enumerate(pairs):
        pltpu.make_async_copy(src, mid, in_sem.at[n]).start()
    for n, (src, mid, out, hot, kind) in enumerate(pairs):
        pltpu.make_async_copy(src, mid, in_sem.at[n]).wait()
        if not hot:
            pltpu.make_async_copy(mid, out(0), out_sem).start()
            continue
        for t in (1, 2):
            filled = slots[me, t - 1] >= 0

            @pl.when(filled)
            def _():
                pltpu.make_async_copy(mid, out(t), out_sem).start()

            @pl.when(jnp.logical_not(filled))
            def _():
                if kind == 0:
                    pltpu.make_async_copy(zero, out(t), out_sem).start()
                else:
                    for h in range(2):
                        pltpu.make_async_copy(zero.at[pl.ds(0, 512)], out(t).at[:, pl.ds(h * 1024, 1024)], out_sem).start()
    for n, (src, mid, out, hot, kind) in enumerate(pairs):
        for t in (1, 2) if hot else (0,):
            pltpu.make_async_copy(mid, out(t), out_sem).wait()


def solution(mesh):
    DMA = pltpu.SemaphoreType.DMA

    def local(gate, up, down, hot_units, slot_map):
        units13 = jax.ShapeDtypeStruct((2, 2048, 1024), BF16)
        unitsd = jax.ShapeDtypeStruct((2, 512, 2048), BF16)
        params = pltpu.CompilerParams(has_side_effects=True, vmem_limit_bytes=48 << 20)
        home13, homed = pl.pallas_call(
            home_kernel,
            out_shape=(units13, unitsd),
            in_specs=[ANY] * 3,
            out_specs=(ANY, ANY),
            scratch_shapes=[
                pltpu.VMEM((2, 2, 2048, 512), BF16),
                pltpu.VMEM((2, 512, 2048), BF16),
                DMA((2, 3)),
                DMA((2, 3)),
                DMA((2, 3)),
            ],
            compiler_params=params,
            name="home",
        )(gate, up, down)

        def hot(unit):
            return pl.pallas_call(
                functools.partial(hot_kernel, unit),
                out_shape=(units13, unitsd),
                in_specs=[ANY] * 3,
                out_specs=(ANY, ANY),
                scratch_shapes=[
                    pltpu.VMEM((2, 2, 2048, 512), BF16),
                    pltpu.VMEM((2, 512, 2048), BF16),
                    DMA((3,)),
                    DMA((2, 3, N)),
                    DMA((2, 3, 2)),
                    DMA((2, 3)),
                    DMA((2, 3)),
                    DMA((2, 3)),
                ],
                compiler_params=params,
                name=f"hot{unit}",
            )

        hot13, hotd = lax.switch(hot_units[0], [hot(u) for u in range(16)], gate, up, down)
        return pl.pallas_call(
            place_kernel,
            out_shape=(
                jax.ShapeDtypeStruct((2, 3, 2048, 1024), BF16),
                jax.ShapeDtypeStruct((2, 3, 512, 2048), BF16),
            ),
            in_specs=[pl.BlockSpec(memory_space=pltpu.SMEM)] + [ANY] * 4,
            out_specs=(ANY, ANY),
            scratch_shapes=[
                [pltpu.VMEM((2, 2048, 1024), BF16)] * 2,
                [pltpu.VMEM((2, 512, 2048), BF16)] * 2,
                pltpu.VMEM((1024, 1024), BF16),
                DMA((12,)),
                DMA,
            ],
            compiler_params=pltpu.CompilerParams(vmem_limit_bytes=48 << 20),
            name="place",
        )(slot_map, home13, homed, hot13, hotd)

    spec = P("stage", "expert")
    out = P(None, ("stage", "expert"))
    return jax.shard_map(local, mesh=mesh, in_specs=(spec, spec, spec, P(), P()), out_specs=(out, out), check_vma=False)
```

time: 552 us -> 246 us (0.45)
  the two profiles are of different devices: /device:TPU:0 before, /device:TPU:5 now
where the time goes in v1:
time: 246 us
  Pallas kernels  244 us (99%)
    pallas_call x1, Pallas kernels, local(): pl.pallas_call(home_kernel, out_shape=(units13, unitsd), in_specs=[ANY] *...  146 us
    pallas_call x1, Pallas kernels, local(): lax.switch(hot_units[0], [hot(u) for u in range(16)], gate, up, down)  81.3 us
    pallas_call x1, Pallas kernels, local(): pl.pallas_call(place_kernel, out_shape=(jax.ShapeDtypeStruct((2, 3, 2048,...  16.4 us

profile of v1, /device:TPU:5, one launch (start us, length us, event | category | flops | bytes accessed | tf_op | source)
XLA Modules:
  0.0 246.2 jit_solution(9129345559528442693)
XLA Ops:
  1.3 0.8 copy.7.slots
  2.0 81.3 %conditional.1 = ((bf16[2,2048,1024]{2,1,0:T(8,128)(2,1)}, bf16[2,512,2048]{2,1,0:T(8,128)(2,1)})) conditional(s32[]{:T(128)} %bitcast, (bf16[1,1,2048,1024]{3,2,1,0:T(8,128)(2,1)}, bf16[1,1,2048,1024]{3,2,1,0:T(8,128)(2,1)}, bf16[1,1,1024,2048]{3,2,1,0:T(8,128)(2,1)}) %tuple.55, ...), branch_computations={%region_0.0_spmd, %region_1.0_spmd, %region_2.0_spmd, %region_3.0_... | conditional | bytes 8 | solution.py:288
  2.0 81.3 %hot2.1 = (bf16[2,2048,1024]{2,1,0:T(8,128)(2,1)}, bf16[2,512,2048]{2,1,0:T(8,128)(2,1)}) custom-call(bf16[1,1,2048,1024]{3,2,1,0:T(8,128)(2,1)} %get-tuple-element.102.gate, bf16[1,1,2048,1024]{3,2,1,0:T(8,128)(2,1)} %get-tuple-element.103.up, bf16[1,1,1024,2048]{3,2,1,0:T(8,128)(2,1)} %get-tuple-element.104.down), custom_call_target="tpu_custom_call" | custom-call | tf_op jit(solution)/shard_map/cond/branch_2_fun/hot2/pallas_call | solution.py:288
  83.4 0.0 copy-start
  83.4 146.4 %home.1 = (bf16[2,2048,1024]{2,1,0:T(8,128)(2,1)}, bf16[2,512,2048]{2,1,0:T(8,128)(2,1)S(1)}) custom-call(bf16[1,1,2048,1024]{3,2,1,0:T(8,128)(2,1)} %gate.1, bf16[1,1,2048,1024]{3,2,1,0:T(8,128)(2,1)} %up.1, bf16[1,1,1024,2048]{3,2,1,0:T(8,128)(2,1)} %down.1), custom_call_target="tpu_custom_call" | custom-call | tf_op jit(solution)/shard_map/home/pallas_call | solution.py:252
  229.8 0.0 copy-done
  229.8 16.4 %place.1 = (bf16[2,3,2048,1024]{3,2,1,0:T(8,128)(2,1)}, bf16[2,3,512,2048]{3,2,1,0:T(8,128)(2,1)}) custom-call(s32[16,2]{1,0:T(8,128)S(1)} %copy.7.slots, bf16[2,2048,1024]{2,1,0:T(8,128)(2,1)} %get-tuple-element.150.home13, bf16[2,512,2048]{2,1,0:T(8,128)(2,1)S(1)} %get-tuple-element.151.homed, bf16[2,2048,1024]{2,1,0:T(8,128)(2,1)S(1)} %copy-done, ...), custom_call_target="tpu_custom_call" | custom-call | tf_op jit(solution)/shard_map/place/pallas_call | solution.py:289
Async XLA Ops:
  83.4 146.4 %copy-start = (bf16[2,2048,1024]{2,1,0:T(8,128)(2,1)S(1)}, bf16[2,2048,1024]{2,1,0:T(8,128)(2,1)}, u32[]{:S(2)}) copy-start(bf16[2,2048,1024]{2,1,0:T(8,128)(2,1)} %get-tuple-element.152.hot13) | copy-start | bytes 25165828

commit v2 on v1

--- a/solution.py
+++ b/solution.py
@@ -22,7 +22,9 @@
     (0, 3, 3, 4, 1, 2, 2, 3),
 )
 CHILDREN = tuple(tuple(tuple(v for v in range(1, 8) if par[v] == r) for r in range(8)) for par in PARENT)
+DEEPEST = max(map(max, DEPTH))
 N = 16
+WINDOW = 3
 
 
 def coords():
@@ -47,76 +49,30 @@
     return out
 
 
-def home_kernel(gate, up, down, home13, homed, vg, vd, load_sem, send_sem, recv_sem):
-    s, a, b, c = coords()
-
-    def source(k, p):
-        if p == 2:
-            return down.at[0, 0, pl.ds(k * 512, 512), :], vd.at[k]
-        return (gate, up)[p].at[0, 0, :, pl.ds(k * 512, 512)], vg.at[k, p]
-
-    def dest(layer, p):
-        return homed.at[layer] if p == 2 else home13.at[layer, :, pl.ds(p * 512, 512)]
-
-    loads = {}
-    for p in range(3):
-        for k in range(2):
-            loads[k, p] = pltpu.make_async_copy(*source(k, p), load_sem.at[k, p])
-            loads[k, p].start()
-    stay = [(s == a) & (a == b) & (b == c) & (c == k) for k in range(2)]
-
-    def send(k, p):
-        return pltpu.make_async_remote_copy(
-            src_ref=source(k, p)[1],
-            dst_ref=dest(s, p),
-            send_sem=send_sem.at[k, p],
-            recv_sem=recv_sem.at[s, p],
-            device_id=dev(a, b, c, k),
-            device_id_type=MESH,
-        )
-
-    for p in range(3):
-        for k in range(2):
-            loads[k, p].wait()
-
-            @pl.when(stay[k])
-            def _():
-                pltpu.make_async_copy(source(k, p)[1], dest(s, p), recv_sem.at[s, p]).start()
-
-            @pl.when(jnp.logical_not(stay[k]))
-            def _():
-                send(k, p).start()
-
-    for p in range(3):
-        for k in range(2):
-
-            @pl.when(jnp.logical_not(stay[k]))
-            def _():
-                send(k, p).wait_send()
-
-    for layer in range(2):
-        for p in range(3):
-            pltpu.make_async_copy(dest(layer, p), dest(layer, p), recv_sem.at[layer, p]).wait()
-
-
-def hot_kernel(unit, gate, up, down, hot13, hotd, vg, vd, load_sem, recv_sem, send_sem, side_send, side_recv, out_sem):
-    e, k = unit // 2, unit % 2
+def move_kernel(unit, gate, up, down, home13, homed, hot13, hotd, vg, vd, load_sem, recv_sem, send_sem, side_send, side_recv, out_sem, home_send, home_recv):
+    e, half = unit // 2, unit % 2
     ra, rb, rc = e // 4, (e // 2) % 2, e % 2
     z, y, x, q = coords()
 
-    def source(p):
-        return down.at[0, 0, pl.ds(k * 512, 512), :] if p == 2 else (gate, up)[p].at[0, 0, :, pl.ds(k * 512, 512)]
+    def source(k, p, i=None):
+        if p == 2:
+            return down.at[0, 0, pl.ds(k * 512, 512), :] if i is None else down.at[0, 0, pl.ds(k * 512 + i * (512 // N), 512 // N), :]
+        cols = pl.ds(k * 512, 512)
+        return (gate, up)[p].at[0, 0, :, cols] if i is None else (gate, up)[p].at[0, 0, pl.ds(i * (2048 // N), 2048 // N), cols]
 
     def held(s, p, i=None):
         if p == 2:
             return vd.at[s] if i is None else vd.at[s, pl.ds(i * (512 // N), 512 // N), :]
         return vg.at[s, p] if i is None else vg.at[s, p, pl.ds(i * (2048 // N), 2048 // N), :]
 
-    def final(s, p, i=None):
+    def place(out13, outd, s, p, i=None):
         if p == 2:
-            return hotd.at[s] if i is None else hotd.at[s, pl.ds(i * (512 // N), 512 // N), :]
+            return outd.at[s] if i is None else outd.at[s, pl.ds(i * (512 // N), 512 // N), :]
         cols = pl.ds(p * 512, 512)
-        return hot13.at[s, :, cols] if i is None else hot13.at[s, pl.ds(i * (2048 // N), 2048 // N), cols]
+        return out13.at[s, :, cols] if i is None else out13.at[s, pl.ds(i * (2048 // N), 2048 // N), cols]
+
+    final = functools.partial(place, hot13, hotd)
+    home = functools.partial(place, home13, homed)
 
     state = []
     for s in range(2):
@@ -131,11 +87,11 @@
         @pl.when(relay & (rel == 0))
         def _():
             for p in range(3):
-                pltpu.make_async_copy(source(p), held(s, p), load_sem.at[p]).start()
-            for p in range(3):
-                pltpu.make_async_copy(source(p), held(s, p), load_sem.at[p]).wait()
-
-    def step(t, carry):
+                pltpu.make_async_copy(source(half, p), held(s, p), load_sem.at[p]).start()
+            for p in range(3):
+                pltpu.make_async_copy(source(half, p), held(s, p), load_sem.at[p]).wait()
+
+    def hot_wave(t):
         for s in range(2):
             rel, relay, fz, fy, fx = state[s]
             for p in range(3):
@@ -175,13 +131,55 @@
                     ).start()
                     pltpu.make_async_copy(held(s, p, i), final(s, p, i), out_sem.at[s, p]).start()
 
+    stay = [(z == y) & (y == x) & (x == q) & (q == k) for k in range(2)]
+
+    def home_copy(k, p, i, slot):
+        return pltpu.make_async_remote_copy(
+            src_ref=source(k, p, i),
+            dst_ref=home(z, p, i),
+            send_sem=home_send.at[k, slot],
+            recv_sem=home_recv.at[z, p],
+            device_id=dev(y, x, q, k),
+            device_id_type=MESH,
+        )
+
+    def step(g, carry):
+        @pl.when(g < N + DEEPEST)
+        def _():
+            hot_wave(g)
+
+        slot = g % WINDOW
+        for k in range(2):
+
+            @pl.when(jnp.logical_not(stay[k]) & (g >= WINDOW))
+            def _():
+                home_copy(k, 0, 0, slot).wait_send()
+
+            for p in range(3):
+
+                @pl.when((g % 3 == p) & jnp.logical_not(stay[k]))
+                def _():
+                    home_copy(k, p, g // 3, slot).start()
+
+                @pl.when((g % 3 == p) & stay[k])
+                def _():
+                    pltpu.make_async_copy(source(k, p, g // 3), home(z, p, g // 3), home_recv.at[z, p]).start()
+
         return carry
 
-    lax.fori_loop(0, N + max(map(max, DEPTH)), step, 0)
+    lax.fori_loop(0, 3 * N, step, 0)
+
+    for k in range(2):
+
+        @pl.when(jnp.logical_not(stay[k]))
+        def _():
+            for slot in range(WINDOW):
+                home_copy(k, 0, 0, slot).wait_send()
 
     for s in range(2):
         rel, relay = state[s][:2]
         for p in range(3):
+            pltpu.make_async_copy(home(s, p), home(s, p), home_recv.at[s, p]).wait()
 
             @pl.when(relay)
             def _():
@@ -249,28 +247,12 @@
         units13 = jax.ShapeDtypeStruct((2, 2048, 1024), BF16)
         unitsd = jax.ShapeDtypeStruct((2, 512, 2048), BF16)
         params = pltpu.CompilerParams(has_side_effects=True, vmem_limit_bytes=48 << 20)
-        home13, homed = pl.pallas_call(
-            home_kernel,
-            out_shape=(units13, unitsd),
-            in_specs=[ANY] * 3,
-            out_specs=(ANY, ANY),
-            scratch_shapes=[
-                pltpu.VMEM((2, 2, 2048, 512), BF16),
-                pltpu.VMEM((2, 512, 2048), BF16),
-                DMA((2, 3)),
-                DMA((2, 3)),
-                DMA((2, 3)),
-            ],
-            compiler_params=params,
-            name="home",
-        )(gate, up, down)
-
-        def hot(unit):
+        def move(unit):
             return pl.pallas_call(
-                functools.partial(hot_kernel, unit),
-                out_shape=(units13, unitsd),
+                functools.partial(move_kernel, unit),
+                out_shape=(units13, unitsd) * 2,
                 in_specs=[ANY] * 3,
-                out_specs=(ANY, ANY),
+                out_specs=(ANY,) * 4,
                 scratch_shapes=[
                     pltpu.VMEM((2, 2, 2048, 512), BF16),
                     pltpu.VMEM((2, 512, 2048), BF16),
@@ -280,12 +262,14 @@
                     DMA((2, 3)),
                     DMA((2, 3)),
                     DMA((2, 3)),
+                    DMA((2, WINDOW)),
+                    DMA((2, 3)),
                 ],
                 compiler_params=params,
-                name=f"hot{unit}",
+                name=f"move{unit}",
             )
 
-        hot13, hotd = lax.switch(hot_units[0], [hot(u) for u in range(16)], gate, up, down)
+        moved = lax.switch(hot_units[0], [move(u) for u in range(16)], gate, up, down)
         return pl.pallas_call(
             place_kernel,
             out_shape=(
@@ -303,7 +287,7 @@
             ],
             compiler_params=pltpu.CompilerParams(vmem_limit_bytes=48 << 20),
             name="place",
-        )(slot_map, home13, homed, hot13, hotd)
+        )(slot_map, *moved)
 
     spec = P("stage", "expert")
     out = P(None, ("stage", "expert"))

time: 246 us -> 342 us (1.39)
  the two profiles are of different devices: /device:TPU:5 before, /device:TPU:15 now
where the time goes in v2:
time: 342 us; the launch traced here: 339 us
  Pallas kernels  336 us (98%)
    pallas_call x1, Pallas kernels, local(): lax.switch(hot_units[0], [move(u) for u in range(16)], gate, up, down)  314 us
    pallas_call x1, Pallas kernels, local(): pl.pallas_call(place_kernel, out_shape=(jax.ShapeDtypeStruct((2, 3, 2048,...  22.4 us

profile of v2, /device:TPU:15, one launch (start us, length us, event | category | flops | bytes accessed | tf_op | source)
XLA Modules:
  0.0 338.6 jit_solution(2280689207012191078)
XLA Ops:
  1.3 0.8 copy.7.slots
  2.0 314.1 %conditional.1 = ((bf16[2,2048,1024]{2,1,0:T(8,128)(2,1)}, bf16[2,512,2048]{2,1,0:T(8,128)(2,1)}, bf16[2,2048,1024]{2,1,0:T(8,128)(2,1)}, bf16[2,512,2048]{2,1,0:T(8,128)(2,1)})) conditional(s32[]{:T(128)} %bitcast, (bf16[1,1,2048,1024]{3,2,1,0:T(8,128)(2,1)}, bf16[1,1,2048,1024]{3,2,1,0:T(8,128)(2,1)}, ...), branch_computations={%region_0.0_spmd, %region_1.0_spmd, %region_2.0_spmd, %region_3.0_... | conditional | bytes 8 | solution.py:272
  2.0 314.1 %move9.1 = (bf16[2,2048,1024]{2,1,0:T(8,128)(2,1)}, bf16[2,512,2048]{2,1,0:T(8,128)(2,1)}, bf16[2,2048,1024]{2,1,0:T(8,128)(2,1)}, bf16[2,512,2048]{2,1,0:T(8,128)(2,1)}) custom-call(bf16[1,1,2048,1024]{3,2,1,0:T(8,128)(2,1)} %get-tuple-element.123.gate, bf16[1,1,2048,1024]{3,2,1,0:T(8,128)(2,1)} %get-tuple-element.124.up, ...), custom_call_target="tpu_custom_call" | custom-call | tf_op jit(solution)/shard_map/cond/branch_9_fun/move9/pallas_call | solution.py:272
  316.2 22.4 %place.1 = (bf16[2,3,2048,1024]{3,2,1,0:T(8,128)(2,1)}, bf16[2,3,512,2048]{3,2,1,0:T(8,128)(2,1)}) custom-call(s32[16,2]{1,0:T(8,128)S(1)} %copy.7.slots, bf16[2,2048,1024]{2,1,0:T(8,128)(2,1)} %get-tuple-element.150.home13, bf16[2,512,2048]{2,1,0:T(8,128)(2,1)} %get-tuple-element.151.homed, bf16[2,2048,1024]{2,1,0:T(8,128)(2,1)} %get-tuple-element.152.hot13, ...), custom_call_target="tpu_custom_call" | custom-call | tf_op jit(solution)/shard_map/place/pallas_call | solution.py:273

commit v3 on v2

--- a/solution.py
+++ b/solution.py
@@ -49,7 +49,7 @@
     return out
 
 
-def move_kernel(unit, gate, up, down, home13, homed, hot13, hotd, vg, vd, load_sem, recv_sem, send_sem, side_send, side_recv, out_sem, home_send, home_recv):
+def move_kernel(unit, gate, up, down, home13, homed, hot13, hotd, vg, vd, sg, sd, load_sem, stage_sem, recv_sem, send_sem, side_send, side_recv, out_sem, home_send, home_recv):
     e, half = unit // 2, unit % 2
     ra, rb, rc = e // 4, (e // 2) % 2, e % 2
     z, y, x, q = coords()
@@ -59,6 +59,11 @@
             return down.at[0, 0, pl.ds(k * 512, 512), :] if i is None else down.at[0, 0, pl.ds(k * 512 + i * (512 // N), 512 // N), :]
         cols = pl.ds(k * 512, 512)
         return (gate, up)[p].at[0, 0, :, cols] if i is None else (gate, up)[p].at[0, 0, pl.ds(i * (2048 // N), 2048 // N), cols]
+
+    def staged(k, p, i=None):
+        if p == 2:
+            return sd.at[k] if i is None else sd.at[k, pl.ds(i * (512 // N), 512 // N), :]
+        return sg.at[k, p] if i is None else sg.at[k, p, pl.ds(i * (2048 // N), 2048 // N), :]
 
     def held(s, p, i=None):
         if p == 2:
@@ -80,6 +85,10 @@
         rel = fz * 4 + fy * 2 + fx
         relay = q == jnp.where(rel == 0, rc, s)
         state.append((rel, relay, fz, fy, fx))
+
+    for p in range(3):
+        for k in range(2):
+            pltpu.make_async_copy(source(k, p), staged(k, p), stage_sem.at[k, p]).start()
 
     for s in range(2):
         rel, relay = state[s][:2]
@@ -135,7 +144,7 @@
 
     def home_copy(k, p, i, slot):
         return pltpu.make_async_remote_copy(
-            src_ref=source(k, p, i),
+            src_ref=staged(k, p, i),
             dst_ref=home(z, p, i),
             send_sem=home_send.at[k, slot],
             recv_sem=home_recv.at[z, p],
@@ -143,6 +152,10 @@
             device_id_type=MESH,
         )
 
+    for p in range(3):
+        for k in range(2):
+            pltpu.make_async_copy(source(k, p), staged(k, p), stage_sem.at[k, p]).wait()
+
     def step(g, carry):
         @pl.when(g < N + DEEPEST)
         def _():
@@ -163,7 +176,7 @@
 
                 @pl.when((g % 3 == p) & stay[k])
                 def _():
-                    pltpu.make_async_copy(source(k, p, g // 3), home(z, p, g // 3), home_recv.at[z, p]).start()
+                    pltpu.make_async_copy(staged(k, p, g // 3), home(z, p, g // 3), home_recv.at[z, p]).start()
 
         return carry
 
@@ -256,7 +269,10 @@
                 scratch_shapes=[
                     pltpu.VMEM((2, 2, 2048, 512), BF16),
                     pltpu.VMEM((2, 512, 2048), BF16),
+                    pltpu.VMEM((2, 2, 2048, 512), BF16),
+                    pltpu.VMEM((2, 512, 2048), BF16),
                     DMA((3,)),
+                    DMA((2, 3)),
                     DMA((2, 3, N)),
                     DMA((2, 3, 2)),
                     DMA((2, 3)),

time: 342 us -> 401 us (1.17)
  the two profiles are of different devices: /device:TPU:15 before, /device:TPU:5 now
where the time goes in v3:
time: 401 us
  Pallas kernels  399 us (100%)
    pallas_call x1, Pallas kernels, local(): lax.switch(hot_units[0], [move(u) for u in range(16)], gate, up, down)  377 us
    pallas_call x1, Pallas kernels, local(): pl.pallas_call(place_kernel, out_shape=(jax.ShapeDtypeStruct((2, 3, 2048,...  22.4 us

profile of v3, /device:TPU:5, one launch (start us, length us, event | category | flops | bytes accessed | tf_op | source)
XLA Modules:
  0.0 401.2 jit_solution(14760324209756646366)
XLA Ops:
  1.3 0.8 copy.7.slots
  2.0 376.8 %conditional.1 = ((bf16[2,2048,1024]{2,1,0:T(8,128)(2,1)}, bf16[2,512,2048]{2,1,0:T(8,128)(2,1)}, bf16[2,2048,1024]{2,1,0:T(8,128)(2,1)}, bf16[2,512,2048]{2,1,0:T(8,128)(2,1)})) conditional(s32[]{:T(128)} %bitcast, (bf16[1,1,2048,1024]{3,2,1,0:T(8,128)(2,1)}, bf16[1,1,2048,1024]{3,2,1,0:T(8,128)(2,1)}, ...), branch_computations={%region_0.0_spmd, %region_1.0_spmd, %region_2.0_spmd, %region_3.0_... | conditional | bytes 8 | solution.py:288
  2.0 376.7 %move9.1 = (bf16[2,2048,1024]{2,1,0:T(8,128)(2,1)}, bf16[2,512,2048]{2,1,0:T(8,128)(2,1)}, bf16[2,2048,1024]{2,1,0:T(8,128)(2,1)}, bf16[2,512,2048]{2,1,0:T(8,128)(2,1)}) custom-call(bf16[1,1,2048,1024]{3,2,1,0:T(8,128)(2,1)} %get-tuple-element.123.gate, bf16[1,1,2048,1024]{3,2,1,0:T(8,128)(2,1)} %get-tuple-element.124.up, ...), custom_call_target="tpu_custom_call" | custom-call | tf_op jit(solution)/shard_map/cond/branch_9_fun/move9/pallas_call | solution.py:288
  378.8 22.4 %place.1 = (bf16[2,3,2048,1024]{3,2,1,0:T(8,128)(2,1)}, bf16[2,3,512,2048]{3,2,1,0:T(8,128)(2,1)}) custom-call(s32[16,2]{1,0:T(8,128)S(1)} %copy.7.slots, bf16[2,2048,1024]{2,1,0:T(8,128)(2,1)} %get-tuple-element.150.home13, bf16[2,512,2048]{2,1,0:T(8,128)(2,1)} %get-tuple-element.151.homed, bf16[2,2048,1024]{2,1,0:T(8,128)(2,1)} %get-tuple-element.152.hot13, ...), custom_call_target="tpu_custom_call" | custom-call | tf_op jit(solution)/shard_map/place/pallas_call | solution.py:289

commit v4 on v2

v4 whole, which is shorter than its diff:
```python
import functools

import jax
import jax.numpy as jnp
from jax import lax
from jax.experimental import pallas as pl
from jax.experimental.pallas import tpu as pltpu
from jax.sharding import PartitionSpec as P

MESH = pl.DeviceIdType.MESH
ANY = pl.BlockSpec(memory_space=pl.ANY)
BF16 = jnp.bfloat16

PARENT = (
    (None, 0, 3, 1, 5, 1, 7, 5),
    (None, 3, 0, 2, 6, 7, 2, 3),
    (None, 5, 6, 7, 0, 4, 4, 6),
)
DEPTH = (
    (0, 1, 3, 2, 3, 2, 4, 3),
    (0, 3, 1, 2, 3, 4, 2, 3),
    (0, 3, 3, 4, 1, 2, 2, 3),
)
CHILDREN = tuple(tuple(tuple(v for v in range(1, 8) if par[v] == r) for r in range(8)) for par in PARENT)
DEEPEST = max(map(max, DEPTH))
N = 16
LAG = 2


def coords():
    z = lax.axis_index("stage")
    j = lax.axis_index("expert")
    return z, j // 4, (j // 2) % 2, j % 2


def dev(z, y, x, q):
    return (z, y * 4 + x * 2 + q)


def flip(v, bit):
    return 1 - v if bit else v


def table(index, values):
    out = jnp.int32(values[0])
    for i, v in enumerate(values[1:], 1):
        if v != values[0]:
            out = jnp.where(index == i, jnp.int32(v), out)
    return out


def roles(s, rb, rc):
    depth, passes, sends = [], [], []
    for p in range(3):
        def sender(r, v):
            x = (r & 1) ^ rb
            return x if r ^ v == 1 else 1 - x

        def entry(r):
            if r == 0:
                return rc
            children = CHILDREN[p][r]
            return sender(r, children[0]) if children else s

        depth.append([LAG * DEPTH[p][r] + (q != entry(r)) for r in range(8) for q in range(2)])
        passes.append([int(q == entry(r)) for r in range(8) for q in range(2)])
        to = [[v * 2 + entry(v) for v in CHILDREN[p][r] if sender(r, v) == q] for r in range(8) for q in range(2)]
        sends.append([[t[m] if len(t) > m else -1 for t in to] for m in range(max(map(len, to)))])
    return depth, passes, sends


def move_kernel(unit, gate, up, down, home13, homed, hot13, hotd, vg, vd, sg, sd, load_sem, stage_sem, recv_sem, send_sem, side_send, out_sem, home_send, home_recv):
    e, half = unit // 2, unit % 2
    ra, rb, rc = e // 4, (e // 2) % 2, e % 2
    z, y, x, q = coords()

    def source(k, p):
        return down.at[0, 0, pl.ds(k * 512, 512), :] if p == 2 else (gate, up)[p].at[0, 0, :, pl.ds(k * 512, 512)]

    def staged(k, p):
        return sd.at[k] if p == 2 else sg.at[k, p]

    def held(s, p, i=None):
        if p == 2:
            return vd.at[s] if i is None else vd.at[s, pl.ds(i * (512 // N), 512 // N), :]
        return vg.at[s, p] if i is None else vg.at[s, p, pl.ds(i * (2048 // N), 2048 // N), :]

    def place(out13, outd, s, p, i=None):
        if p == 2:
            return outd.at[s] if i is None else outd.at[s, pl.ds(i * (512 // N), 512 // N), :]
        cols = pl.ds(p * 512, 512)
        return out13.at[s, :, cols] if i is None else out13.at[s, pl.ds(i * (2048 // N), 2048 // N), cols]

    final = functools.partial(place, hot13, hotd)
    home = functools.partial(place, home13, homed)

    trees = [roles(s, rb, rc) for s in range(2)]
    rels = [flip(z, s) * 4 + flip(y, ra) * 2 + flip(x, rb) for s in range(2)]
    spots = [rel * 2 + q for rel in rels]
    stay = [(z == y) & (y == x) & (x == q) & (q == k) for k in range(2)]

    def stage(k, p):
        return pltpu.make_async_copy(source(k, p), staged(k, p), stage_sem.at[k, p])

    def load(s, p):
        return pltpu.make_async_copy(source(half, p), held(s, p), load_sem.at[p])

    def home_copy(k, p):
        return pltpu.make_async_remote_copy(
            src_ref=staged(k, p),
            dst_ref=home(z, p),
            send_sem=home_send.at[k, p],
            recv_sem=home_recv.at[z, p],
            device_id=dev(y, x, q, k),
            device_id_type=MESH,
        )

    for s in range(2):

        @pl.when(spots[s] == rc)
        def _():
            for p in range(3):
                load(s, p).start()

    for p in range(3):
        for k in range(2):
            stage(k, p).start()

    for p in range(3):
        for k in range(2):
            stage(k, p).wait()

            @pl.when(stay[k])
            def _():
                pltpu.make_async_copy(staged(k, p), home(z, p), home_recv.at[z, p]).start()

            @pl.when(jnp.logical_not(stay[k]))
            def _():
                home_copy(k, p).start()

    for s in range(2):

        @pl.when(spots[s] == rc)
        def _():
            for p in range(3):
                load(s, p).wait()

    def wave(t, carry):
        for s in range(2):
            spot = spots[s]
            depth, passes, sends = trees[s]
            for p in range(3):
                i = t - table(spot, depth[p])

                @pl.when((i >= 0) & (i < N))
                def _():
                    @pl.when(spot != rc)
                    def _():
                        pltpu.make_async_copy(held(s, p, i), held(s, p, i), recv_sem.at[s, p, i]).wait()

                    def forward(to, sem):
                        return pltpu.make_async_remote_copy(
                            src_ref=held(s, p, i),
                            dst_ref=held(s, p, i),
                            send_sem=sem,
                            recv_sem=recv_sem.at[s, p, i],
                            device_id=to,
                            device_id_type=MESH,
                        )

                    for m, row in enumerate(sends[p]):
                        child = table(spot, row)

                        @pl.when(child >= 0)
                        def _():
                            to = dev(flip(child // 8, s), flip((child // 4) % 2, ra), flip((child // 2) % 2, rb), child % 2)
                            forward(to, send_sem.at[s, p, m]).start()

                    @pl.when(table(spot, passes[p]) == 1)
                    def _():
                        forward(dev(z, y, x, 1 - q), side_send.at[s, p]).start()

                    pltpu.make_async_copy(held(s, p, i), final(s, p, i), out_sem.at[s, p]).start()

        return carry

    lax.fori_loop(0, N + LAG * DEEPEST + 1, wave, 0)

    for s in range(2):
        spot = spots[s]
        _, passes, sends = trees[s]
        for p in range(3):
            for m, row in enumerate(sends[p]):

                @pl.when(table(spot, row) >= 0)
                def _():
                    pltpu.make_async_copy(held(s, p), held(s, p), send_sem.at[s, p, m]).wait()

            @pl.when(table(spot, passes[p]) == 1)
            def _():
                pltpu.make_async_copy(held(s, p), held(s, p), side_send.at[s, p]).wait()

            pltpu.make_async_copy(held(s, p), final(s, p), out_sem.at[s, p]).wait()

    for k in range(2):

        @pl.when(jnp.logical_not(stay[k]))
        def _():
            for p in range(3):
                home_copy(k, p).wait_send()

    for s in range(2):
        for p in range(3):
            pltpu.make_async_copy(home(s, p), home(s, p), home_recv.at[s, p]).wait()


def place_kernel(slots, home13, homed, hot13, hotd, out13, outd, va, vb, zero, in_sem, out_sem):
    me = lax.axis_index("stage") * 8 + lax.axis_index("expert")
    vah, vaH = va
    vbh, vbH = vb
    zero[...] = jnp.zeros_like(zero)
    pairs = []
    for g in range(4):
        layer, r = g // 2, g % 2
        rows = pl.ds(r * 1024, 1024)
        pairs.append((home13.at[layer, rows], vah.at[layer, rows], lambda t, layer=layer, rows=rows: out13.at[layer, t, rows], False, 0))
        pairs.append((hot13.at[layer, rows], vaH.at[layer, rows], lambda t, layer=layer, rows=rows: out13.at[layer, t, rows], True, 0))
    for layer in range(2):
        pairs.append((homed.at[layer], vbh.at[layer], lambda t, layer=layer: outd.at[layer, t], False, 1))
        pairs.append((hotd.at[layer], vbH.at[layer], lambda t, layer=layer: outd.at[layer, t], True, 1))
    for n, (src, mid, out, hot, kind) in enumerate(pairs):
        pltpu.make_async_copy(src, mid, in_sem.at[n]).start()
    for n, (src, mid, out, hot, kind) in enumerate(pairs):
        pltpu.make_async_copy(src, mid, in_sem.at[n]).wait()
        if not hot:
            pltpu.make_async_copy(mid, out(0), out_sem).start()
            continue
        for t in (1, 2):
            filled = slots[me, t - 1] >= 0

            @pl.when(filled)
            def _():
                pltpu.make_async_copy(mid, out(t), out_sem).start()

            @pl.when(jnp.logical_not(filled))
            def _():
                if kind == 0:
                    pltpu.make_async_copy(zero, out(t), out_sem).start()
                else:
                    for h in range(2):
                        pltpu.make_async_copy(zero.at[pl.ds(0, 512)], out(t).at[:, pl.ds(h * 1024, 1024)], out_sem).start()
    for n, (src, mid, out, hot, kind) in enumerate(pairs):
        for t in (1, 2) if hot else (0,):
            pltpu.make_async_copy(mid, out(t), out_sem).wait()


def solution(mesh):
    DMA = pltpu.SemaphoreType.DMA

    def local(gate, up, down, hot_units, slot_map):
        units13 = jax.ShapeDtypeStruct((2, 2048, 1024), BF16)
        unitsd = jax.ShapeDtypeStruct((2, 512, 2048), BF16)
        params = pltpu.CompilerParams(has_side_effects=True, vmem_limit_bytes=48 << 20)
        def move(unit):
            return pl.pallas_call(
                functools.partial(move_kernel, unit),
                out_shape=(units13, unitsd) * 2,
                in_specs=[ANY] * 3,
                out_specs=(ANY,) * 4,
                scratch_shapes=[
                    pltpu.VMEM((2, 2, 2048, 512), BF16),
                    pltpu.VMEM((2, 512, 2048), BF16),
                    pltpu.VMEM((2, 2, 2048, 512), BF16),
                    pltpu.VMEM((2, 512, 2048), BF16),
                    DMA((3,)),
                    DMA((2, 3)),
                    DMA((2, 3, N)),
                    DMA((2, 3, 2)),
                    DMA((2, 3)),
                    DMA((2, 3)),
                    DMA((2, 3)),
                    DMA((2, 3)),
                ],
                compiler_params=params,
                name=f"move{unit}",
            )

        moved = lax.switch(hot_units[0], [move(u) for u in range(16)], gate, up, down)
        return pl.pallas_call(
            place_kernel,
            out_shape=(
                jax.ShapeDtypeStruct((2, 3, 2048, 1024), BF16),
                jax.ShapeDtypeStruct((2, 3, 512, 2048), BF16),
            ),
            in_specs=[pl.BlockSpec(memory_space=pltpu.SMEM)] + [ANY] * 4,
            out_specs=(ANY, ANY),
            scratch_shapes=[
                [pltpu.VMEM((2, 2048, 1024), BF16)] * 2,
                [pltpu.VMEM((2, 512, 2048), BF16)] * 2,
                pltpu.VMEM((1024, 1024), BF16),
                DMA((12,)),
                DMA,
            ],
            compiler_params=pltpu.CompilerParams(vmem_limit_bytes=48 << 20),
            name="place",
        )(slot_map, *moved)

    spec = P("stage", "expert")
    out = P(None, ("stage", "expert"))
    return jax.shard_map(local, mesh=mesh, in_specs=(spec, spec, spec, P(), P()), out_specs=(out, out), check_vma=False)
```

time: 342 us -> 231 us (0.68)
  the two profiles are of different devices: /device:TPU:15 before, /device:TPU:0 now
where the time goes in v4:
time: 231 us; the launch traced here: 230 us
  Pallas kernels  228 us (99%)
    pallas_call x1, Pallas kernels, local(): lax.switch(hot_units[0], [move(u) for u in range(16)], gate, up, down)  205 us
    pallas_call x1, Pallas kernels, local(): pl.pallas_call(place_kernel, out_shape=(jax.ShapeDtypeStruct((2, 3, 2048,...  22.4 us

profile of v4, /device:TPU:0, one launch (start us, length us, event | category | flops | bytes accessed | tf_op | source)
XLA Modules:
  0.0 230.2 jit_solution(9937226795732508913)
XLA Ops:
  1.3 0.8 copy.7.slots
  2.0 205.5 %conditional.1 = ((bf16[2,2048,1024]{2,1,0:T(8,128)(2,1)}, bf16[2,512,2048]{2,1,0:T(8,128)(2,1)}, bf16[2,2048,1024]{2,1,0:T(8,128)(2,1)}, bf16[2,512,2048]{2,1,0:T(8,128)(2,1)})) conditional(s32[]{:T(128)} %bitcast, (bf16[1,1,2048,1024]{3,2,1,0:T(8,128)(2,1)}, bf16[1,1,2048,1024]{3,2,1,0:T(8,128)(2,1)}, ...), branch_computations={%region_0.0_spmd, %region_1.0_spmd, %region_2.0_spmd, %region_3.0_... | conditional | bytes 8 | solution.py:288
  2.0 205.3 %move3.1 = (bf16[2,2048,1024]{2,1,0:T(8,128)(2,1)}, bf16[2,512,2048]{2,1,0:T(8,128)(2,1)}, bf16[2,2048,1024]{2,1,0:T(8,128)(2,1)}, bf16[2,512,2048]{2,1,0:T(8,128)(2,1)}) custom-call(bf16[1,1,2048,1024]{3,2,1,0:T(8,128)(2,1)} %get-tuple-element.105.gate, bf16[1,1,2048,1024]{3,2,1,0:T(8,128)(2,1)} %get-tuple-element.106.up, ...), custom_call_target="tpu_custom_call" | custom-call | tf_op jit(solution)/shard_map/cond/branch_3_fun/move3/pallas_call | solution.py:288
  207.6 22.4 %place.1 = (bf16[2,3,2048,1024]{3,2,1,0:T(8,128)(2,1)}, bf16[2,3,512,2048]{3,2,1,0:T(8,128)(2,1)}) custom-call(s32[16,2]{1,0:T(8,128)S(1)} %copy.7.slots, bf16[2,2048,1024]{2,1,0:T(8,128)(2,1)} %get-tuple-element.150.home13, bf16[2,512,2048]{2,1,0:T(8,128)(2,1)} %get-tuple-element.151.homed, bf16[2,2048,1024]{2,1,0:T(8,128)(2,1)} %get-tuple-element.152.hot13, ...), custom_call_target="tpu_custom_call" | custom-call | tf_op jit(solution)/shard_map/place/pallas_call | solution.py:289

commit v5 on v4

--- a/solution.py
+++ b/solution.py
@@ -23,8 +23,8 @@
 )
 CHILDREN = tuple(tuple(tuple(v for v in range(1, 8) if par[v] == r) for r in range(8)) for par in PARENT)
 DEEPEST = max(map(max, DEPTH))
-N = 16
-LAG = 2
+N = 32
+LAG = 3
 
 
 def coords():
@@ -69,7 +69,7 @@
     return depth, passes, sends
 
 
-def move_kernel(unit, gate, up, down, home13, homed, hot13, hotd, vg, vd, sg, sd, load_sem, stage_sem, recv_sem, send_sem, side_send, out_sem, home_send, home_recv):
+def move_kernel(unit, gate, up, down, home13, homed, vg, vd, sg, sd, load_sem, stage_sem, recv_sem, send_sem, side_send, home_send, home_recv):
     e, half = unit // 2, unit % 2
     ra, rb, rc = e // 4, (e // 2) % 2, e % 2
     z, y, x, q = coords()
@@ -85,14 +85,8 @@
             return vd.at[s] if i is None else vd.at[s, pl.ds(i * (512 // N), 512 // N), :]
         return vg.at[s, p] if i is None else vg.at[s, p, pl.ds(i * (2048 // N), 2048 // N), :]
 
-    def place(out13, outd, s, p, i=None):
-        if p == 2:
-            return outd.at[s] if i is None else outd.at[s, pl.ds(i * (512 // N), 512 // N), :]
-        cols = pl.ds(p * 512, 512)
-        return out13.at[s, :, cols] if i is None else out13.at[s, pl.ds(i * (2048 // N), 2048 // N), cols]
-
-    final = functools.partial(place, hot13, hotd)
-    home = functools.partial(place, home13, homed)
+    def home(s, p):
+        return homed.at[s] if p == 2 else home13.at[s, :, pl.ds(p * 512, 512)]
 
     trees = [roles(s, rb, rc) for s in range(2)]
     rels = [flip(z, s) * 4 + flip(y, ra) * 2 + flip(x, rb) for s in range(2)]
@@ -180,8 +174,6 @@
                     def _():
                         forward(dev(z, y, x, 1 - q), side_send.at[s, p]).start()
 
-                    pltpu.make_async_copy(held(s, p, i), final(s, p, i), out_sem.at[s, p]).start()
-
         return carry
 
     lax.fori_loop(0, N + LAG * DEEPEST + 1, wave, 0)
@@ -200,8 +192,6 @@
             def _():
                 pltpu.make_async_copy(held(s, p), held(s, p), side_send.at[s, p]).wait()
 
-            pltpu.make_async_copy(held(s, p), final(s, p), out_sem.at[s, p]).wait()
-
     for k in range(2):
 
         @pl.when(jnp.logical_not(stay[k]))
@@ -214,64 +204,58 @@
             pltpu.make_async_copy(home(s, p), home(s, p), home_recv.at[s, p]).wait()
 
 
-def place_kernel(slots, home13, homed, hot13, hotd, out13, outd, va, vb, zero, in_sem, out_sem):
+def place_kernel(slots, home13, homed, hot13, hotd, out13, outd, zero, sem):
     me = lax.axis_index("stage") * 8 + lax.axis_index("expert")
-    vah, vaH = va
-    vbh, vbH = vb
     zero[...] = jnp.zeros_like(zero)
-    pairs = []
-    for g in range(4):
-        layer, r = g // 2, g % 2
-        rows = pl.ds(r * 1024, 1024)
-        pairs.append((home13.at[layer, rows], vah.at[layer, rows], lambda t, layer=layer, rows=rows: out13.at[layer, t, rows], False, 0))
-        pairs.append((hot13.at[layer, rows], vaH.at[layer, rows], lambda t, layer=layer, rows=rows: out13.at[layer, t, rows], True, 0))
+
+    def pieces(layer, slot):
+        return out13.at[layer, slot, :, pl.ds(0, 512)], out13.at[layer, slot, :, pl.ds(512, 512)], outd.at[layer, slot]
+
     for layer in range(2):
-        pairs.append((homed.at[layer], vbh.at[layer], lambda t, layer=layer: outd.at[layer, t], False, 1))
-        pairs.append((hotd.at[layer], vbH.at[layer], lambda t, layer=layer: outd.at[layer, t], True, 1))
-    for n, (src, mid, out, hot, kind) in enumerate(pairs):
-        pltpu.make_async_copy(src, mid, in_sem.at[n]).start()
-    for n, (src, mid, out, hot, kind) in enumerate(pairs):
-        pltpu.make_async_copy(src, mid, in_sem.at[n]).wait()
-        if not hot:
-            pltpu.make_async_copy(mid, out(0), out_sem).start()
-            continue
-        for t in (1, 2):
-            filled = slots[me, t - 1] >= 0
+        pltpu.make_async_copy(home13.at[layer], out13.at[layer, 0], sem).start()
+        pltpu.make_async_copy(homed.at[layer], outd.at[layer, 0], sem).start()
+        for t in range(2):
+            filled = slots[me, t] >= 0
+            to = pieces(layer, t + 1)
 
             @pl.when(filled)
             def _():
-                pltpu.make_async_copy(mid, out(t), out_sem).start()
+                for p in range(3):
+                    pltpu.make_async_copy(hotd.at[layer] if p == 2 else hot13.at[layer, p], to[p], sem).start()
 
             @pl.when(jnp.logical_not(filled))
             def _():
-                if kind == 0:
-                    pltpu.make_async_copy(zero, out(t), out_sem).start()
-                else:
-                    for h in range(2):
-                        pltpu.make_async_copy(zero.at[pl.ds(0, 512)], out(t).at[:, pl.ds(h * 1024, 1024)], out_sem).start()
-    for n, (src, mid, out, hot, kind) in enumerate(pairs):
-        for t in (1, 2) if hot else (0,):
-            pltpu.make_async_copy(mid, out(t), out_sem).wait()
+                for h in range(4):
+                    pltpu.make_async_copy(zero, out13.at[layer, t + 1, pl.ds(h * 512, 512)], sem).start()
+                for h in range(2):
+                    pltpu.make_async_copy(zero, outd.at[layer, t + 1, :, pl.ds(h * 1024, 1024)], sem).start()
+
+    for layer in range(2):
+        for t in range(3):
+            pltpu.make_async_copy(home13.at[layer], out13.at[layer, t], sem).wait()
+            pltpu.make_async_copy(homed.at[layer], outd.at[layer, t], sem).wait()
 
 
 def solution(mesh):
     DMA = pltpu.SemaphoreType.DMA
 
+    VMEM = pl.BlockSpec(memory_space=pltpu.VMEM)
+
     def local(gate, up, down, hot_units, slot_map):
-        units13 = jax.ShapeDtypeStruct((2, 2048, 1024), BF16)
-        unitsd = jax.ShapeDtypeStruct((2, 512, 2048), BF16)
-        params = pltpu.CompilerParams(has_side_effects=True, vmem_limit_bytes=48 << 20)
-        def move(unit):
-            return pl.pallas_call(
+        def branch(unit, gate, up, down, slot_map):
+            moved = pl.pallas_call(
                 functools.partial(move_kernel, unit),
-                out_shape=(units13, unitsd) * 2,
+                out_shape=(
+                    pltpu.VMEM((2, 2048, 1024), BF16),
+                    pltpu.VMEM((2, 512, 2048), BF16),
+                    pltpu.VMEM((2, 2, 2048, 512), BF16),
+                    pltpu.VMEM((2, 512, 2048), BF16),
+                ),
                 in_specs=[ANY] * 3,
-                out_specs=(ANY,) * 4,
+                out_specs=(VMEM,) * 4,
                 scratch_shapes=[
                     pltpu.VMEM((2, 2, 2048, 512), BF16),
                     pltpu.VMEM((2, 512, 2048), BF16),
-                    pltpu.VMEM((2, 2, 2048, 512), BF16),
-                    pltpu.VMEM((2, 512, 2048), BF16),
                     DMA((3,)),
                     DMA((2, 3)),
                     DMA((2, 3, N)),
@@ -279,31 +263,24 @@
                     DMA((2, 3)),
                     DMA((2, 3)),
                     DMA((2, 3)),
-                    DMA((2, 3)),
                 ],
-                compiler_params=params,
+                compiler_params=pltpu.CompilerParams(has_side_effects=True, vmem_limit_bytes=14 << 20),
                 name=f"move{unit}",
-            )
-
-        moved = lax.switch(hot_units[0], [move(u) for u in range(16)], gate, up, down)
-        return pl.pallas_call(
-            place_kernel,
-            out_shape=(
-                jax.ShapeDtypeStruct((2, 3, 2048, 1024), BF16),
-                jax.ShapeDtypeStruct((2, 3, 512, 2048), BF16),
-            ),
-            in_specs=[pl.BlockSpec(memory_space=pltpu.SMEM)] + [ANY] * 4,
-            out_specs=(ANY, ANY),
-            scratch_shapes=[
-                [pltpu.VMEM((2, 2048, 1024), BF16)] * 2,
-                [pltpu.VMEM((2, 512, 2048), BF16)] * 2,
-                pltpu.VMEM((1024, 1024), BF16),
-                DMA((12,)),
-                DMA,
-            ],
-            compiler_params=pltpu.CompilerParams(vmem_limit_bytes=48 << 20),
-            name="place",
-        )(slot_map, *moved)
+            )(gate, up, down)
+            return pl.pallas_call(
+                place_kernel,
+                out_shape=(
+                    jax.ShapeDtypeStruct((2, 3, 2048, 1024), BF16),
+                    jax.ShapeDtypeStruct((2, 3, 512, 2048), BF16),
+                ),
+                in_specs=[pl.BlockSpec(memory_space=pltpu.SMEM)] + [VMEM] * 4,
+                out_specs=(ANY, ANY),
+                scratch_shapes=[pltpu.VMEM((512, 1024), BF16), DMA],
+                compiler_params=pltpu.CompilerParams(vmem_limit_bytes=4 << 20),
+                name="place",
+            )(slot_map, *moved)
+
+        return lax.switch(hot_units[0], [functools.partial(branch, u) for u in range(16)], gate, up, down, slot_map)
 
     spec = P("stage", "expert")
     out = P(None, ("stage", "expert"))

time: 231 us -> 216 us (0.935)
  Pallas kernels: 228 us -> 213 us
    pallas_call x2, Pallas kernels: 228 us -> 213 us  [the longest x1 201 us: branch(): pl.pallas_call(functools.partial(move_kernel, unit), out_shape=(pltpu.VME...]
where the time goes in v5:
time: 216 us
  Pallas kernels  213 us (99%)
    pallas_call x1, Pallas kernels, branch(): pl.pallas_call(functools.partial(move_kernel, unit), out_shape=(pltpu.VME...  201 us
    pallas_call x1, Pallas kernels, branch(): pl.pallas_call(place_kernel, out_shape=(jax.ShapeDtypeStruct((2, 3, 2048,...  12.8 us

profile of v5, /device:TPU:0, one launch (start us, length us, event | category | flops | bytes accessed | tf_op | source)
XLA Modules:
  0.0 215.9 jit_solution(9101185165977091122)
XLA Ops:
  1.3 214.4 %conditional.1 = ((bf16[2,3,2048,1024]{3,2,1,0:T(8,128)(2,1)}, bf16[2,3,512,2048]{3,2,1,0:T(8,128)(2,1)})) conditional(s32[]{:T(128)} %bitcast, (bf16[1,1,2048,1024]{3,2,1,0:T(8,128)(2,1)}, bf16[1,1,2048,1024]{3,2,1,0:T(8,128)(2,1)}, bf16[1,1,1024,2048]{3,2,1,0:T(8,128)(2,1)}, s32[16,2]{0,1:T(2,128)}) %tuple.55, ...), branch_computations={%region_0.0_spmd, %region_1.0_spmd, %region_2.0_spmd, %region_3.0_... | conditional | bytes 264 | solution.py:283
  1.5 0.8 copy.48.slots
  2.3 200.6 %move9.1 = (bf16[2,2048,1024]{2,1,0:T(8,128)(2,1)S(1)}, bf16[2,512,2048]{2,1,0:T(8,128)(2,1)S(1)}, bf16[2,2,2048,512]{3,2,1,0:T(8,128)(2,1)S(1)}, bf16[2,512,2048]{2,1,0:T(8,128)(2,1)S(1)}) custom-call(bf16[1,1,2048,1024]{3,2,1,0:T(8,128)(2,1)} %get-tuple-element.201.gate, bf16[1,1,2048,1024]{3,2,1,0:T(8,128)(2,1)} %get-tuple-element.202.up, ...), custom_call_target="tpu_custom_call" | custom-call | tf_op jit(solution)/shard_map/cond/branch_9_fun/move9/pallas_call | solution.py:246
  202.9 12.8 %place.25 = (bf16[2,3,2048,1024]{3,2,1,0:T(8,128)(2,1)}, bf16[2,3,512,2048]{3,2,1,0:T(8,128)(2,1)}) custom-call(s32[16,2]{1,0:T(8,128)S(1)} %copy.48.slots, bf16[2,2048,1024]{2,1,0:T(8,128)(2,1)S(1)} %get-tuple-element.204.home13, bf16[2,512,2048]{2,1,0:T(8,128)(2,1)S(1)} %get-tuple-element.205.homed, ...), custom_call_target="tpu_custom_call" | custom-call | tf_op jit(solution)/shard_map/cond/branch_9_fun/place/pallas_call | solution.py:270

commit v6 on v5

--- a/solution.py
+++ b/solution.py
@@ -23,7 +23,7 @@
 )
 CHILDREN = tuple(tuple(tuple(v for v in range(1, 8) if par[v] == r) for r in range(8)) for par in PARENT)
 DEEPEST = max(map(max, DEPTH))
-N = 32
+N = 64
 LAG = 3
 
 

time: 216 us -> 254 us (1.18)
  Pallas kernels: 213 us -> 252 us
    pallas_call x1, Pallas kernels: 201 us -> 239 us  [branch(): pl.pallas_call(functools.partial(move_kernel, unit), out_shape=(pltpu.VME...]
where the time goes in v6:
time: 254 us; the launch traced here: 255 us
  Pallas kernels  252 us (99%)
    pallas_call x1, Pallas kernels, branch(): pl.pallas_call(functools.partial(move_kernel, unit), out_shape=(pltpu.VME...  239 us
    pallas_call x1, Pallas kernels, branch(): pl.pallas_call(place_kernel, out_shape=(jax.ShapeDtypeStruct((2, 3, 2048,...  12.8 us

profile of v6, /device:TPU:0, one launch (start us, length us, event | category | flops | bytes accessed | tf_op | source)
XLA Modules:
  0.0 254.6 jit_solution(16096238052178710136)
XLA Ops:
  1.3 253.1 %conditional.1 = ((bf16[2,3,2048,1024]{3,2,1,0:T(8,128)(2,1)}, bf16[2,3,512,2048]{3,2,1,0:T(8,128)(2,1)})) conditional(s32[]{:T(128)} %bitcast, (bf16[1,1,2048,1024]{3,2,1,0:T(8,128)(2,1)}, bf16[1,1,2048,1024]{3,2,1,0:T(8,128)(2,1)}, bf16[1,1,1024,2048]{3,2,1,0:T(8,128)(2,1)}, s32[16,2]{0,1:T(2,128)}) %tuple.55, ...), branch_computations={%region_0.0_spmd, %region_1.0_spmd, %region_2.0_spmd, %region_3.0_... | conditional | bytes 264 | solution.py:283
  1.5 0.8 copy.51.slots
  2.3 238.7 %move12.1 = (bf16[2,2048,1024]{2,1,0:T(8,128)(2,1)S(1)}, bf16[2,512,2048]{2,1,0:T(8,128)(2,1)S(1)}, bf16[2,2,2048,512]{3,2,1,0:T(8,128)(2,1)S(1)}, bf16[2,512,2048]{2,1,0:T(8,128)(2,1)S(1)}) custom-call(bf16[1,1,2048,1024]{3,2,1,0:T(8,128)(2,1)} %get-tuple-element.225.gate, bf16[1,1,2048,1024]{3,2,1,0:T(8,128)(2,1)} %get-tuple-element.226.up, ...), custom_call_target="tpu_custom_call" | custom-call | tf_op jit(solution)/shard_map/cond/branch_12_fun/move12/pallas_call | solution.py:246
  241.0 12.8 %place.28 = (bf16[2,3,2048,1024]{3,2,1,0:T(8,128)(2,1)}, bf16[2,3,512,2048]{3,2,1,0:T(8,128)(2,1)}) custom-call(s32[16,2]{1,0:T(8,128)S(1)} %copy.51.slots, bf16[2,2048,1024]{2,1,0:T(8,128)(2,1)S(1)} %get-tuple-element.228.home13, bf16[2,512,2048]{2,1,0:T(8,128)(2,1)S(1)} %get-tuple-element.229.homed, ...), custom_call_target="tpu_custom_call" | custom-call | tf_op jit(solution)/shard_map/cond/branch_12_fun/place/pallas_call | solution.py:270

commit v7 on v6

--- a/solution.py
+++ b/solution.py
@@ -24,7 +24,8 @@
 CHILDREN = tuple(tuple(tuple(v for v in range(1, 8) if par[v] == r) for r in range(8)) for par in PARENT)
 DEEPEST = max(map(max, DEPTH))
 N = 64
-LAG = 3
+HOME_AT = 64
+LAG = 6
 
 
 def coords():
@@ -120,18 +121,6 @@
         for k in range(2):
             stage(k, p).start()
 
-    for p in range(3):
-        for k in range(2):
-            stage(k, p).wait()
-
-            @pl.when(stay[k])
-            def _():
-                pltpu.make_async_copy(staged(k, p), home(z, p), home_recv.at[z, p]).start()
-
-            @pl.when(jnp.logical_not(stay[k]))
-            def _():
-                home_copy(k, p).start()
-
     for s in range(2):
 
         @pl.when(spots[s] == rc)
@@ -139,7 +128,24 @@
             for p in range(3):
                 load(s, p).wait()
 
+    def start_home():
+        for p in range(3):
+            for k in range(2):
+                stage(k, p).wait()
+
+                @pl.when(stay[k])
+                def _():
+                    pltpu.make_async_copy(staged(k, p), home(z, p), home_recv.at[z, p]).start()
+
+                @pl.when(jnp.logical_not(stay[k]))
+                def _():
+                    home_copy(k, p).start()
+
     def wave(t, carry):
+        @pl.when(t == HOME_AT)
+        def _():
+            start_home()
+
         for s in range(2):
             spot = spots[s]
             depth, passes, sends = trees[s]

time: 254 us -> 228 us (0.90)
  Pallas kernels: 252 us -> 225 us
    pallas_call x1, Pallas kernels: 239 us -> 212 us  [branch(): pl.pallas_call(functools.partial(move_kernel, unit), out_shape=(pltpu.VME...]
where the time goes in v7:
time: 228 us
  Pallas kernels  225 us (99%)
    pallas_call x1, Pallas kernels, branch(): pl.pallas_call(functools.partial(move_kernel, unit), out_shape=(pltpu.VME...  212 us
    pallas_call x1, Pallas kernels, branch(): pl.pallas_call(place_kernel, out_shape=(jax.ShapeDtypeStruct((2, 3, 2048,...  12.8 us

profile of v7, /device:TPU:0, one launch (start us, length us, event | category | flops | bytes accessed | tf_op | source)
XLA Modules:
  0.0 227.7 jit_solution(12924932596917387526)
XLA Ops:
  1.3 226.2 %conditional.1 = ((bf16[2,3,2048,1024]{3,2,1,0:T(8,128)(2,1)}, bf16[2,3,512,2048]{3,2,1,0:T(8,128)(2,1)})) conditional(s32[]{:T(128)} %bitcast, (bf16[1,1,2048,1024]{3,2,1,0:T(8,128)(2,1)}, bf16[1,1,2048,1024]{3,2,1,0:T(8,128)(2,1)}, bf16[1,1,1024,2048]{3,2,1,0:T(8,128)(2,1)}, s32[16,2]{0,1:T(2,128)}) %tuple.55, ...), branch_computations={%region_0.0_spmd, %region_1.0_spmd, %region_2.0_spmd, %region_3.0_... | conditional | bytes 264 | solution.py:289
  1.3 0.8 copy.43.slots
  2.1 211.8 %move4.1 = (bf16[2,2048,1024]{2,1,0:T(8,128)(2,1)S(1)}, bf16[2,512,2048]{2,1,0:T(8,128)(2,1)S(1)}, bf16[2,2,2048,512]{3,2,1,0:T(8,128)(2,1)S(1)}, bf16[2,512,2048]{2,1,0:T(8,128)(2,1)S(1)}) custom-call(bf16[1,1,2048,1024]{3,2,1,0:T(8,128)(2,1)} %get-tuple-element.161.gate, bf16[1,1,2048,1024]{3,2,1,0:T(8,128)(2,1)} %get-tuple-element.162.up, ...), custom_call_target="tpu_custom_call" | custom-call | tf_op jit(solution)/shard_map/cond/branch_4_fun/move4/pallas_call | solution.py:252
  213.9 12.8 %place.20 = (bf16[2,3,2048,1024]{3,2,1,0:T(8,128)(2,1)}, bf16[2,3,512,2048]{3,2,1,0:T(8,128)(2,1)}) custom-call(s32[16,2]{1,0:T(8,128)S(1)} %copy.43.slots, bf16[2,2048,1024]{2,1,0:T(8,128)(2,1)S(1)} %get-tuple-element.164.home13, bf16[2,512,2048]{2,1,0:T(8,128)(2,1)S(1)} %get-tuple-element.165.homed, ...), custom_call_target="tpu_custom_call" | custom-call | tf_op jit(solution)/shard_map/cond/branch_4_fun/place/pallas_call | solution.py:276

commit v8 on v7

--- a/solution.py
+++ b/solution.py
@@ -23,9 +23,9 @@
 )
 CHILDREN = tuple(tuple(tuple(v for v in range(1, 8) if par[v] == r) for r in range(8)) for par in PARENT)
 DEEPEST = max(map(max, DEPTH))
-N = 64
-HOME_AT = 64
-LAG = 6
+N = 32
+HOME_AT = 10
+LAG = 3
 
 
 def coords():

time: 228 us -> 231 us (1.013)
  Pallas kernels: 225 us -> 230 us
    pallas_call x1, Pallas kernels: 212 us -> 217 us  [branch(): pl.pallas_call(functools.partial(move_kernel, unit), out_shape=(pltpu.VME...]
where the time goes in v8:
time: 231 us; the launch traced here: 232 us
  Pallas kernels  230 us (100%)
    pallas_call x1, Pallas kernels, branch(): pl.pallas_call(functools.partial(move_kernel, unit), out_shape=(pltpu.VME...  217 us
    pallas_call x1, Pallas kernels, branch(): pl.pallas_call(place_kernel, out_shape=(jax.ShapeDtypeStruct((2, 3, 2048,...  12.8 us

profile of v8, /device:TPU:0, one launch (start us, length us, event | category | flops | bytes accessed | tf_op | source)
XLA Modules:
  0.0 232.1 jit_solution(7636844330458235471)
XLA Ops:
  1.3 230.6 %conditional.1 = ((bf16[2,3,2048,1024]{3,2,1,0:T(8,128)(2,1)}, bf16[2,3,512,2048]{3,2,1,0:T(8,128)(2,1)})) conditional(s32[]{:T(128)} %bitcast, (bf16[1,1,2048,1024]{3,2,1,0:T(8,128)(2,1)}, bf16[1,1,2048,1024]{3,2,1,0:T(8,128)(2,1)}, bf16[1,1,1024,2048]{3,2,1,0:T(8,128)(2,1)}, s32[16,2]{0,1:T(2,128)}) %tuple.55, ...), branch_computations={%region_0.0_spmd, %region_1.0_spmd, %region_2.0_spmd, %region_3.0_... | conditional | bytes 264 | solution.py:289
  1.5 0.8 copy.51.slots
  2.3 216.8 %move12.1 = (bf16[2,2048,1024]{2,1,0:T(8,128)(2,1)S(1)}, bf16[2,512,2048]{2,1,0:T(8,128)(2,1)S(1)}, bf16[2,2,2048,512]{3,2,1,0:T(8,128)(2,1)S(1)}, bf16[2,512,2048]{2,1,0:T(8,128)(2,1)S(1)}) custom-call(bf16[1,1,2048,1024]{3,2,1,0:T(8,128)(2,1)} %get-tuple-element.225.gate, bf16[1,1,2048,1024]{3,2,1,0:T(8,128)(2,1)} %get-tuple-element.226.up, ...), custom_call_target="tpu_custom_call" | custom-call | tf_op jit(solution)/shard_map/cond/branch_12_fun/move12/pallas_call | solution.py:252
  219.1 12.8 %place.28 = (bf16[2,3,2048,1024]{3,2,1,0:T(8,128)(2,1)}, bf16[2,3,512,2048]{3,2,1,0:T(8,128)(2,1)}) custom-call(s32[16,2]{1,0:T(8,128)S(1)} %copy.51.slots, bf16[2,2048,1024]{2,1,0:T(8,128)(2,1)S(1)} %get-tuple-element.228.home13, bf16[2,512,2048]{2,1,0:T(8,128)(2,1)S(1)} %get-tuple-element.229.homed, ...), custom_call_target="tpu_custom_call" | custom-call | tf_op jit(solution)/shard_map/cond/branch_12_fun/place/pallas_call | solution.py:276

commit v9 on v8

--- a/solution.py
+++ b/solution.py
@@ -23,9 +23,9 @@
 )
 CHILDREN = tuple(tuple(tuple(v for v in range(1, 8) if par[v] == r) for r in range(8)) for par in PARENT)
 DEEPEST = max(map(max, DEPTH))
-N = 32
-HOME_AT = 10
-LAG = 3
+N = 16
+HOME_AT = 0
+LAG = 2
 
 
 def coords():

time: 231 us -> 226 us (0.978)
  Pallas kernels: 230 us -> 223 us
    pallas_call x1, Pallas kernels: 217 us -> 211 us  [branch(): pl.pallas_call(functools.partial(move_kernel, unit), out_shape=(pltpu.VME...]
where the time goes in v9:
time: 226 us
  Pallas kernels  223 us (99%)
    pallas_call x1, Pallas kernels, branch(): pl.pallas_call(functools.partial(move_kernel, unit), out_shape=(pltpu.VME...  211 us
    pallas_call x1, Pallas kernels, branch(): pl.pallas_call(place_kernel, out_shape=(jax.ShapeDtypeStruct((2, 3, 2048,...  12.8 us

profile of v9, /device:TPU:0, one launch (start us, length us, event | category | flops | bytes accessed | tf_op | source)
XLA Modules:
  0.0 226.0 jit_solution(4105179939311732070)
XLA Ops:
  1.3 224.5 %conditional.1 = ((bf16[2,3,2048,1024]{3,2,1,0:T(8,128)(2,1)}, bf16[2,3,512,2048]{3,2,1,0:T(8,128)(2,1)})) conditional(s32[]{:T(128)} %bitcast, (bf16[1,1,2048,1024]{3,2,1,0:T(8,128)(2,1)}, bf16[1,1,2048,1024]{3,2,1,0:T(8,128)(2,1)}, bf16[1,1,1024,2048]{3,2,1,0:T(8,128)(2,1)}, s32[16,2]{0,1:T(2,128)}) %tuple.55, ...), branch_computations={%region_0.0_spmd, %region_1.0_spmd, %region_2.0_spmd, %region_3.0_... | conditional | bytes 264 | solution.py:289
  1.3 0.8 copy.44.slots
  2.1 210.6 %move5.1 = (bf16[2,2048,1024]{2,1,0:T(8,128)(2,1)S(1)}, bf16[2,512,2048]{2,1,0:T(8,128)(2,1)S(1)}, bf16[2,2,2048,512]{3,2,1,0:T(8,128)(2,1)S(1)}, bf16[2,512,2048]{2,1,0:T(8,128)(2,1)S(1)}) custom-call(bf16[1,1,2048,1024]{3,2,1,0:T(8,128)(2,1)} %get-tuple-element.169.gate, bf16[1,1,2048,1024]{3,2,1,0:T(8,128)(2,1)} %get-tuple-element.170.up, ...), custom_call_target="tpu_custom_call" | custom-call | tf_op jit(solution)/shard_map/cond/branch_5_fun/move5/pallas_call | solution.py:252
  212.7 12.8 %place.21 = (bf16[2,3,2048,1024]{3,2,1,0:T(8,128)(2,1)}, bf16[2,3,512,2048]{3,2,1,0:T(8,128)(2,1)}) custom-call(s32[16,2]{1,0:T(8,128)S(1)} %copy.44.slots, bf16[2,2048,1024]{2,1,0:T(8,128)(2,1)S(1)} %get-tuple-element.172.home13, bf16[2,512,2048]{2,1,0:T(8,128)(2,1)S(1)} %get-tuple-element.173.homed, ...), custom_call_target="tpu_custom_call" | custom-call | tf_op jit(solution)/shard_map/cond/branch_5_fun/place/pallas_call | solution.py:276

commit v10 on v9

--- a/solution.py
+++ b/solution.py
@@ -23,8 +23,8 @@
 )
 CHILDREN = tuple(tuple(tuple(v for v in range(1, 8) if par[v] == r) for r in range(8)) for par in PARENT)
 DEEPEST = max(map(max, DEPTH))
-N = 16
-HOME_AT = 0
+N = 32
+HOME_AT = 2
 LAG = 2
 
 

time: 226 us -> 240 us (1.062)
  Pallas kernels: 223 us -> 238 us
    pallas_call x1, Pallas kernels: 211 us -> 225 us  [branch(): pl.pallas_call(functools.partial(move_kernel, unit), out_shape=(pltpu.VME...]
where the time goes in v10:
time: 240 us
  Pallas kernels  238 us (99%)
    pallas_call x1, Pallas kernels, branch(): pl.pallas_call(functools.partial(move_kernel, unit), out_shape=(pltpu.VME...  225 us
    pallas_call x1, Pallas kernels, branch(): pl.pallas_call(place_kernel, out_shape=(jax.ShapeDtypeStruct((2, 3, 2048,...  12.8 us

profile of v10, /device:TPU:0, one launch (start us, length us, event | category | flops | bytes accessed | tf_op | source)
XLA Modules:
  0.0 240.4 jit_solution(5308447971960433711)
XLA Ops:
  1.3 238.9 %conditional.1 = ((bf16[2,3,2048,1024]{3,2,1,0:T(8,128)(2,1)}, bf16[2,3,512,2048]{3,2,1,0:T(8,128)(2,1)})) conditional(s32[]{:T(128)} %bitcast, (bf16[1,1,2048,1024]{3,2,1,0:T(8,128)(2,1)}, bf16[1,1,2048,1024]{3,2,1,0:T(8,128)(2,1)}, bf16[1,1,1024,2048]{3,2,1,0:T(8,128)(2,1)}, s32[16,2]{0,1:T(2,128)}) %tuple.55, ...), branch_computations={%region_0.0_spmd, %region_1.0_spmd, %region_2.0_spmd, %region_3.0_... | conditional | bytes 264 | solution.py:289
  1.3 0.8 copy.41.slots
  2.1 225.1 %move2.1 = (bf16[2,2048,1024]{2,1,0:T(8,128)(2,1)S(1)}, bf16[2,512,2048]{2,1,0:T(8,128)(2,1)S(1)}, bf16[2,2,2048,512]{3,2,1,0:T(8,128)(2,1)S(1)}, bf16[2,512,2048]{2,1,0:T(8,128)(2,1)S(1)}) custom-call(bf16[1,1,2048,1024]{3,2,1,0:T(8,128)(2,1)} %get-tuple-element.145.gate, bf16[1,1,2048,1024]{3,2,1,0:T(8,128)(2,1)} %get-tuple-element.146.up, ...), custom_call_target="tpu_custom_call" | custom-call | tf_op jit(solution)/shard_map/cond/branch_2_fun/move2/pallas_call | solution.py:252
  227.2 12.8 %place.18 = (bf16[2,3,2048,1024]{3,2,1,0:T(8,128)(2,1)}, bf16[2,3,512,2048]{3,2,1,0:T(8,128)(2,1)}) custom-call(s32[16,2]{1,0:T(8,128)S(1)} %copy.41.slots, bf16[2,2048,1024]{2,1,0:T(8,128)(2,1)S(1)} %get-tuple-element.148.home13, bf16[2,512,2048]{2,1,0:T(8,128)(2,1)S(1)} %get-tuple-element.149.homed, ...), custom_call_target="tpu_custom_call" | custom-call | tf_op jit(solution)/shard_map/cond/branch_2_fun/place/pallas_call | solution.py:276

commit v11 on v10

--- a/solution.py
+++ b/solution.py
@@ -24,8 +24,8 @@
 CHILDREN = tuple(tuple(tuple(v for v in range(1, 8) if par[v] == r) for r in range(8)) for par in PARENT)
 DEEPEST = max(map(max, DEPTH))
 N = 32
-HOME_AT = 2
-LAG = 2
+HOME_AT = 0
+LAG = 5
 
 
 def coords():

time: 240 us -> 219 us (0.912); the launches traced: 240 us -> 215 us
  Pallas kernels: 238 us -> 213 us
    pallas_call x1, Pallas kernels: 225 us -> 200 us  [branch(): pl.pallas_call(functools.partial(move_kernel, unit), out_shape=(pltpu.VME...]
where the time goes in v11:
time: 219 us; the launch traced here: 215 us
  Pallas kernels  213 us (97%)
    pallas_call x1, Pallas kernels, branch(): pl.pallas_call(functools.partial(move_kernel, unit), out_shape=(pltpu.VME...  200 us
    pallas_call x1, Pallas kernels, branch(): pl.pallas_call(place_kernel, out_shape=(jax.ShapeDtypeStruct((2, 3, 2048,...  12.8 us

profile of v11, /device:TPU:0, one launch (start us, length us, event | category | flops | bytes accessed | tf_op | source)
XLA Modules:
  0.0 215.5 jit_solution(3642291137967287899)
XLA Ops:
  1.3 214.0 %conditional.1 = ((bf16[2,3,2048,1024]{3,2,1,0:T(8,128)(2,1)}, bf16[2,3,512,2048]{3,2,1,0:T(8,128)(2,1)})) conditional(s32[]{:T(128)} %bitcast, (bf16[1,1,2048,1024]{3,2,1,0:T(8,128)(2,1)}, bf16[1,1,2048,1024]{3,2,1,0:T(8,128)(2,1)}, bf16[1,1,1024,2048]{3,2,1,0:T(8,128)(2,1)}, s32[16,2]{0,1:T(2,128)}) %tuple.55, ...), branch_computations={%region_0.0_spmd, %region_1.0_spmd, %region_2.0_spmd, %region_3.0_... | conditional | bytes 264 | solution.py:289
  1.3 0.8 copy.42.slots
  2.1 200.2 %move3.1 = (bf16[2,2048,1024]{2,1,0:T(8,128)(2,1)S(1)}, bf16[2,512,2048]{2,1,0:T(8,128)(2,1)S(1)}, bf16[2,2,2048,512]{3,2,1,0:T(8,128)(2,1)S(1)}, bf16[2,512,2048]{2,1,0:T(8,128)(2,1)S(1)}) custom-call(bf16[1,1,2048,1024]{3,2,1,0:T(8,128)(2,1)} %get-tuple-element.153.gate, bf16[1,1,2048,1024]{3,2,1,0:T(8,128)(2,1)} %get-tuple-element.154.up, ...), custom_call_target="tpu_custom_call" | custom-call | tf_op jit(solution)/shard_map/cond/branch_3_fun/move3/pallas_call | solution.py:252
  202.3 12.8 %place.19 = (bf16[2,3,2048,1024]{3,2,1,0:T(8,128)(2,1)}, bf16[2,3,512,2048]{3,2,1,0:T(8,128)(2,1)}) custom-call(s32[16,2]{1,0:T(8,128)S(1)} %copy.42.slots, bf16[2,2048,1024]{2,1,0:T(8,128)(2,1)S(1)} %get-tuple-element.156.home13, bf16[2,512,2048]{2,1,0:T(8,128)(2,1)S(1)} %get-tuple-element.157.homed, ...), custom_call_target="tpu_custom_call" | custom-call | tf_op jit(solution)/shard_map/cond/branch_3_fun/place/pallas_call | solution.py:276

commit v12 on v11

--- a/solution.py
+++ b/solution.py
@@ -24,8 +24,8 @@
 CHILDREN = tuple(tuple(tuple(v for v in range(1, 8) if par[v] == r) for r in range(8)) for par in PARENT)
 DEEPEST = max(map(max, DEPTH))
 N = 32
-HOME_AT = 0
-LAG = 5
+HOME_AT = 3
+LAG = 4
 
 
 def coords():
@@ -120,6 +120,18 @@
     for p in range(3):
         for k in range(2):
             stage(k, p).start()
+
+    barrier = pltpu.get_barrier_semaphore()
+
+    def greet(d, carry):
+        @pl.when((d // 8 != z) | (d % 8 != y * 4 + x * 2 + q))
+        def _():
+            pl.semaphore_signal(barrier, inc=1, device_id=(d // 8, d % 8), device_id_type=MESH)
+
+        return carry
+
+    lax.fori_loop(0, 16, greet, 0)
+    pl.semaphore_wait(barrier, 15)
 
     for s in range(2):
 
@@ -270,7 +282,7 @@
                     DMA((2, 3)),
                     DMA((2, 3)),
                 ],
-                compiler_params=pltpu.CompilerParams(has_side_effects=True, vmem_limit_bytes=14 << 20),
+                compiler_params=pltpu.CompilerParams(has_side_effects=True, collective_id=0, vmem_limit_bytes=14 << 20),
                 name=f"move{unit}",
             )(gate, up, down)
             return pl.pallas_call(

time: 219 us -> 216 us (0.986); the launches traced: 215 us -> 216 us
  no operation moved by 1% of the time
where the time goes in v12:
time: 216 us
  Pallas kernels  214 us (99%)
    pallas_call x1, Pallas kernels, branch(): pl.pallas_call(functools.partial(move_kernel, unit), out_shape=(pltpu.VME...  201 us
    pallas_call x1, Pallas kernels, branch(): pl.pallas_call(place_kernel, out_shape=(jax.ShapeDtypeStruct((2, 3, 2048,...  12.8 us

profile of v12, /device:TPU:0, one launch (start us, length us, event | category | flops | bytes accessed | tf_op | source)
XLA Modules:
  0.0 216.4 jit_solution(16577256455307259108)
XLA Ops:
  1.3 215.0 %conditional.1 = ((bf16[2,3,2048,1024]{3,2,1,0:T(8,128)(2,1)}, bf16[2,3,512,2048]{3,2,1,0:T(8,128)(2,1)})) conditional(s32[]{:T(128)} %bitcast, (bf16[1,1,2048,1024]{3,2,1,0:T(8,128)(2,1)}, bf16[1,1,2048,1024]{3,2,1,0:T(8,128)(2,1)}, bf16[1,1,1024,2048]{3,2,1,0:T(8,128)(2,1)}, s32[16,2]{0,1:T(2,128)}) %tuple.55, ...), branch_computations={%region_0.0_spmd, %region_1.0_spmd, %region_2.0_spmd, %region_3.0_... | conditional | bytes 264 | solution.py:301
  1.5 0.8 copy.49.slots
  2.3 201.1 %move10.1 = (bf16[2,2048,1024]{2,1,0:T(8,128)(2,1)S(1)}, bf16[2,512,2048]{2,1,0:T(8,128)(2,1)S(1)}, bf16[2,2,2048,512]{3,2,1,0:T(8,128)(2,1)S(1)}, bf16[2,512,2048]{2,1,0:T(8,128)(2,1)S(1)}) custom-call(bf16[1,1,2048,1024]{3,2,1,0:T(8,128)(2,1)} %get-tuple-element.209.gate, bf16[1,1,2048,1024]{3,2,1,0:T(8,128)(2,1)} %get-tuple-element.210.up, ...), custom_call_target="tpu_custom_call" | custom-call | tf_op jit(solution)/shard_map/cond/branch_10_fun/move10/pallas_call | solution.py:264
  203.4 12.8 %place.26 = (bf16[2,3,2048,1024]{3,2,1,0:T(8,128)(2,1)}, bf16[2,3,512,2048]{3,2,1,0:T(8,128)(2,1)}) custom-call(s32[16,2]{1,0:T(8,128)S(1)} %copy.49.slots, bf16[2,2048,1024]{2,1,0:T(8,128)(2,1)S(1)} %get-tuple-element.212.home13, bf16[2,512,2048]{2,1,0:T(8,128)(2,1)S(1)} %get-tuple-element.213.homed, ...), custom_call_target="tpu_custom_call" | custom-call | tf_op jit(solution)/shard_map/cond/branch_10_fun/place/pallas_call | solution.py:288

commit v13 on v12

--- a/solution.py
+++ b/solution.py
@@ -24,7 +24,7 @@
 CHILDREN = tuple(tuple(tuple(v for v in range(1, 8) if par[v] == r) for r in range(8)) for par in PARENT)
 DEEPEST = max(map(max, DEPTH))
 N = 32
-HOME_AT = 3
+HOME_AT = 6
 LAG = 4
 
 
@@ -130,8 +130,9 @@
 
         return carry
 
-    lax.fori_loop(0, 16, greet, 0)
-    pl.semaphore_wait(barrier, 15)
+    with jax.named_scope("greet"):
+        lax.fori_loop(0, 16, greet, 0)
+        pl.semaphore_wait(barrier, 15)
 
     for s in range(2):
 
@@ -194,32 +195,36 @@
 
         return carry
 
-    lax.fori_loop(0, N + LAG * DEEPEST + 1, wave, 0)
-
-    for s in range(2):
-        spot = spots[s]
-        _, passes, sends = trees[s]
-        for p in range(3):
-            for m, row in enumerate(sends[p]):
-
-                @pl.when(table(spot, row) >= 0)
+    with jax.named_scope("waves"):
+        lax.fori_loop(0, N + LAG * DEEPEST + 1, wave, 0)
+
+    with jax.named_scope("hot_sent"):
+        for s in range(2):
+            spot = spots[s]
+            _, passes, sends = trees[s]
+            for p in range(3):
+                for m, row in enumerate(sends[p]):
+
+                    @pl.when(table(spot, row) >= 0)
+                    def _():
+                        pltpu.make_async_copy(held(s, p), held(s, p), send_sem.at[s, p, m]).wait()
+
+                @pl.when(table(spot, passes[p]) == 1)
                 def _():
-                    pltpu.make_async_copy(held(s, p), held(s, p), send_sem.at[s, p, m]).wait()
-
-            @pl.when(table(spot, passes[p]) == 1)
+                    pltpu.make_async_copy(held(s, p), held(s, p), side_send.at[s, p]).wait()
+
+    with jax.named_scope("home_sent"):
+        for k in range(2):
+
+            @pl.when(jnp.logical_not(stay[k]))
             def _():
-                pltpu.make_async_copy(held(s, p), held(s, p), side_send.at[s, p]).wait()
-
-    for k in range(2):
-
-        @pl.when(jnp.logical_not(stay[k]))
-        def _():
-            for p in range(3):
-                home_copy(k, p).wait_send()
-
-    for s in range(2):
-        for p in range(3):
-            pltpu.make_async_copy(home(s, p), home(s, p), home_recv.at[s, p]).wait()
+                for p in range(3):
+                    home_copy(k, p).wait_send()
+
+    with jax.named_scope("home_here"):
+        for s in range(2):
+            for p in range(3):
+                pltpu.make_async_copy(home(s, p), home(s, p), home_recv.at[s, p]).wait()
 
 
 def place_kernel(slots, home13, homed, hot13, hotd, out13, outd, zero, sem):

time: 216 us -> 222 us (1.028)
  Pallas kernels: 214 us -> 220 us
    pallas_call x1, Pallas kernels: 201 us -> 207 us  [branch(): pl.pallas_call(functools.partial(move_kernel, unit), out_shape=(pltpu.VME...]
where the time goes in v13:
time: 222 us
  Pallas kernels  220 us (99%)
    pallas_call x1, Pallas kernels, branch(): pl.pallas_call(functools.partial(move_kernel, unit), out_shape=(pltpu.VME...  207 us
    pallas_call x1, Pallas kernels, branch(): pl.pallas_call(place_kernel, out_shape=(jax.ShapeDtypeStruct((2, 3, 2048,...  12.8 us

profile of v13, /device:TPU:0, one launch (start us, length us, event | category | flops | bytes accessed | tf_op | source)
XLA Modules:
  0.0 222.2 jit_solution(11569043335424849381)
XLA Ops:
  1.3 220.8 %conditional.1 = ((bf16[2,3,2048,1024]{3,2,1,0:T(8,128)(2,1)}, bf16[2,3,512,2048]{3,2,1,0:T(8,128)(2,1)})) conditional(s32[]{:T(128)} %bitcast, (bf16[1,1,2048,1024]{3,2,1,0:T(8,128)(2,1)}, bf16[1,1,2048,1024]{3,2,1,0:T(8,128)(2,1)}, bf16[1,1,1024,2048]{3,2,1,0:T(8,128)(2,1)}, s32[16,2]{0,1:T(2,128)}) %tuple.55, ...), branch_computations={%region_0.0_spmd, %region_1.0_spmd, %region_2.0_spmd, %region_3.0_... | conditional | bytes 264 | solution.py:306
  1.5 0.8 copy.47.slots
  2.2 207.0 %move8.1 = (bf16[2,2048,1024]{2,1,0:T(8,128)(2,1)S(1)}, bf16[2,512,2048]{2,1,0:T(8,128)(2,1)S(1)}, bf16[2,2,2048,512]{3,2,1,0:T(8,128)(2,1)S(1)}, bf16[2,512,2048]{2,1,0:T(8,128)(2,1)S(1)}) custom-call(bf16[1,1,2048,1024]{3,2,1,0:T(8,128)(2,1)} %get-tuple-element.193.gate, bf16[1,1,2048,1024]{3,2,1,0:T(8,128)(2,1)} %get-tuple-element.194.up, ...), custom_call_target="tpu_custom_call" | custom-call | tf_op jit(solution)/shard_map/cond/branch_8_fun/move8/pallas_call | solution.py:269
  209.2 12.8 %place.24 = (bf16[2,3,2048,1024]{3,2,1,0:T(8,128)(2,1)}, bf16[2,3,512,2048]{3,2,1,0:T(8,128)(2,1)}) custom-call(s32[16,2]{1,0:T(8,128)S(1)} %copy.47.slots, bf16[2,2048,1024]{2,1,0:T(8,128)(2,1)S(1)} %get-tuple-element.196.home13, bf16[2,512,2048]{2,1,0:T(8,128)(2,1)S(1)} %get-tuple-element.197.homed, ...), custom_call_target="tpu_custom_call" | custom-call | tf_op jit(solution)/shard_map/cond/branch_8_fun/place/pallas_call | solution.py:293

commit v14 on v12

--- a/solution.py
+++ b/solution.py
@@ -24,8 +24,8 @@
 CHILDREN = tuple(tuple(tuple(v for v in range(1, 8) if par[v] == r) for r in range(8)) for par in PARENT)
 DEEPEST = max(map(max, DEPTH))
 N = 32
-HOME_AT = 3
-LAG = 4
+HOME_AT = 4
+LAG = 3
 
 
 def coords():
@@ -222,8 +222,10 @@
             pltpu.make_async_copy(home(s, p), home(s, p), home_recv.at[s, p]).wait()
 
 
-def place_kernel(slots, home13, homed, hot13, hotd, out13, outd, zero, sem):
+def place_kernel(slot_map, home13, homed, hot13, hotd, out13, outd, slots, zero, slots_sem, sem):
     me = lax.axis_index("stage") * 8 + lax.axis_index("expert")
+    fetch = pltpu.make_async_copy(slot_map, slots, slots_sem)
+    fetch.start()
     zero[...] = jnp.zeros_like(zero)
 
     def pieces(layer, slot):
@@ -232,6 +234,9 @@
     for layer in range(2):
         pltpu.make_async_copy(home13.at[layer], out13.at[layer, 0], sem).start()
         pltpu.make_async_copy(homed.at[layer], outd.at[layer, 0], sem).start()
+
+    fetch.wait()
+    for layer in range(2):
         for t in range(2):
             filled = slots[me, t] >= 0
             to = pieces(layer, t + 1)
@@ -291,9 +296,9 @@
                     jax.ShapeDtypeStruct((2, 3, 2048, 1024), BF16),
                     jax.ShapeDtypeStruct((2, 3, 512, 2048), BF16),
                 ),
-                in_specs=[pl.BlockSpec(memory_space=pltpu.SMEM)] + [VMEM] * 4,
+                in_specs=[ANY] + [VMEM] * 4,
                 out_specs=(ANY, ANY),
-                scratch_shapes=[pltpu.VMEM((512, 1024), BF16), DMA],
+                scratch_shapes=[pltpu.SMEM((16, 2), jnp.int32), pltpu.VMEM((512, 1024), BF16), DMA, DMA],
                 compiler_params=pltpu.CompilerParams(vmem_limit_bytes=4 << 20),
                 name="place",
             )(slot_map, *moved)

time: 216 us -> 223 us (1.032)
  Pallas kernels: 214 us -> 220 us
    pallas_call x1, Pallas kernels: 201 us -> 208 us  [branch(): pl.pallas_call(functools.partial(move_kernel, unit), out_shape=(pltpu.VME...]
where the time goes in v14:
time: 223 us; the launch traced here: 222 us
  Pallas kernels  220 us (99%)
    pallas_call x1, Pallas kernels, branch(): pl.pallas_call(functools.partial(move_kernel, unit), out_shape=(pltpu.VME...  208 us
    pallas_call x1, Pallas kernels, branch(): pl.pallas_call(place_kernel, out_shape=(jax.ShapeDtypeStruct((2, 3, 2048,...  12.2 us

profile of v14, /device:TPU:0, one launch (start us, length us, event | category | flops | bytes accessed | tf_op | source)
XLA Modules:
  0.0 222.5 jit_solution(17787705644843838691)
XLA Ops:
  1.3 221.0 %conditional.1 = ((bf16[2,3,2048,1024]{3,2,1,0:T(8,128)(2,1)}, bf16[2,3,512,2048]{3,2,1,0:T(8,128)(2,1)})) conditional(s32[]{:T(128)} %bitcast, (bf16[1,1,2048,1024]{3,2,1,0:T(8,128)(2,1)}, bf16[1,1,2048,1024]{3,2,1,0:T(8,128)(2,1)}, bf16[1,1,1024,2048]{3,2,1,0:T(8,128)(2,1)}, s32[16,2]{0,1:T(2,128)}) %tuple.55, ...), branch_computations={%region_0.0_spmd, %region_1.0_spmd, %region_2.0_spmd, %region_3.0_... | conditional | bytes 264 | solution.py:306
  1.3 0.8 copy.43.slot_map
  2.1 207.9 %move4.1 = (bf16[2,2048,1024]{2,1,0:T(8,128)(2,1)S(1)}, bf16[2,512,2048]{2,1,0:T(8,128)(2,1)S(1)}, bf16[2,2,2048,512]{3,2,1,0:T(8,128)(2,1)S(1)}, bf16[2,512,2048]{2,1,0:T(8,128)(2,1)S(1)}) custom-call(bf16[1,1,2048,1024]{3,2,1,0:T(8,128)(2,1)} %get-tuple-element.161.gate, bf16[1,1,2048,1024]{3,2,1,0:T(8,128)(2,1)} %get-tuple-element.162.up, ...), custom_call_target="tpu_custom_call" | custom-call | tf_op jit(solution)/shard_map/cond/branch_4_fun/move4/pallas_call | solution.py:269
  209.9 12.2 %place.20 = (bf16[2,3,2048,1024]{3,2,1,0:T(8,128)(2,1)}, bf16[2,3,512,2048]{3,2,1,0:T(8,128)(2,1)}) custom-call(s32[16,2]{1,0:T(8,128)S(1)} %copy.43.slot_map, bf16[2,2048,1024]{2,1,0:T(8,128)(2,1)S(1)} %get-tuple-element.164.home13, bf16[2,512,2048]{2,1,0:T(8,128)(2,1)S(1)} %get-tuple-element.165.homed, ...), custom_call_target="tpu_custom_call" | custom-call | tf_op jit(solution)/shard_map/cond/branch_4_fun/place/pallas_call | solution.py:293

commit v15 on v14

--- a/solution.py
+++ b/solution.py
@@ -24,8 +24,8 @@
 CHILDREN = tuple(tuple(tuple(v for v in range(1, 8) if par[v] == r) for r in range(8)) for par in PARENT)
 DEEPEST = max(map(max, DEPTH))
 N = 32
-HOME_AT = 4
-LAG = 3
+HOME_AT = 3
+LAG = 4
 
 
 def coords():
@@ -92,7 +92,11 @@
     trees = [roles(s, rb, rc) for s in range(2)]
     rels = [flip(z, s) * 4 + flip(y, ra) * 2 + flip(x, rb) for s in range(2)]
     spots = [rel * 2 + q for rel in rels]
-    stay = [(z == y) & (y == x) & (x == q) & (q == k) for k in range(2)]
+    holder = (y == ra) & (x == rb) & (q == rc)
+    due = [jnp.logical_not(holder) if k == half else (z >= 0) for k in range(2)]
+    same = [(z == y) & (y == x) & (x == q) & (q == k) for k in range(2)]
+    stay = [due[k] & same[k] for k in range(2)]
+    leave = [due[k] & jnp.logical_not(same[k]) for k in range(2)]
 
     def stage(k, p):
         return pltpu.make_async_copy(source(k, p), staged(k, p), stage_sem.at[k, p])
@@ -149,7 +153,7 @@
                 def _():
                     pltpu.make_async_copy(staged(k, p), home(z, p), home_recv.at[z, p]).start()
 
-                @pl.when(jnp.logical_not(stay[k]))
+                @pl.when(leave[k])
                 def _():
                     home_copy(k, p).start()
 
@@ -212,17 +216,19 @@
 
     for k in range(2):
 
-        @pl.when(jnp.logical_not(stay[k]))
+        @pl.when(leave[k])
         def _():
             for p in range(3):
                 home_copy(k, p).wait_send()
 
-    for s in range(2):
-        for p in range(3):
-            pltpu.make_async_copy(home(s, p), home(s, p), home_recv.at[s, p]).wait()
-
-
-def place_kernel(slot_map, home13, homed, hot13, hotd, out13, outd, slots, zero, slots_sem, sem):
+    @pl.when(jnp.logical_not((z == ra) & (y == rb) & (x == rc) & (q == half)))
+    def _():
+        for s in range(2):
+            for p in range(3):
+                pltpu.make_async_copy(home(s, p), home(s, p), home_recv.at[s, p]).wait()
+
+
+def place_kernel(unit, slot_map, home13, homed, hot13, hotd, out13, outd, slots, zero, slots_sem, sem):
     me = lax.axis_index("stage") * 8 + lax.axis_index("expert")
     fetch = pltpu.make_async_copy(slot_map, slots, slots_sem)
     fetch.start()
@@ -231,20 +237,30 @@
     def pieces(layer, slot):
         return out13.at[layer, slot, :, pl.ds(0, 512)], out13.at[layer, slot, :, pl.ds(512, 512)], outd.at[layer, slot]
 
-    for layer in range(2):
-        pltpu.make_async_copy(home13.at[layer], out13.at[layer, 0], sem).start()
-        pltpu.make_async_copy(homed.at[layer], outd.at[layer, 0], sem).start()
+    def place_hot(layer, slot):
+        to = pieces(layer, slot)
+        for p in range(3):
+            pltpu.make_async_copy(hotd.at[layer] if p == 2 else hot13.at[layer, p], to[p], sem).start()
+
+    @pl.when(me != unit)
+    def _():
+        for layer in range(2):
+            pltpu.make_async_copy(home13.at[layer], out13.at[layer, 0], sem).start()
+            pltpu.make_async_copy(homed.at[layer], outd.at[layer, 0], sem).start()
+
+    @pl.when(me == unit)
+    def _():
+        for layer in range(2):
+            place_hot(layer, 0)
 
     fetch.wait()
     for layer in range(2):
         for t in range(2):
             filled = slots[me, t] >= 0
-            to = pieces(layer, t + 1)
 
             @pl.when(filled)
             def _():
-                for p in range(3):
-                    pltpu.make_async_copy(hotd.at[layer] if p == 2 else hot13.at[layer, p], to[p], sem).start()
+                place_hot(layer, t + 1)
 
             @pl.when(jnp.logical_not(filled))
             def _():
@@ -291,12 +307,12 @@
                 name=f"move{unit}",
             )(gate, up, down)
             return pl.pallas_call(
-                place_kernel,
+                functools.partial(place_kernel, unit),
                 out_shape=(
                     jax.ShapeDtypeStruct((2, 3, 2048, 1024), BF16),
                     jax.ShapeDtypeStruct((2, 3, 512, 2048), BF16),
                 ),
-                in_specs=[ANY] + [VMEM] * 4,
+                in_specs=[pl.BlockSpec(memory_space=pltpu.HBM)] + [VMEM] * 4,
                 out_specs=(ANY, ANY),
                 scratch_shapes=[pltpu.SMEM((16, 2), jnp.int32), pltpu.VMEM((512, 1024), BF16), DMA, DMA],
                 compiler_params=pltpu.CompilerParams(vmem_limit_bytes=4 << 20),

time: 223 us -> 215 us (0.964)
  Pallas kernels: 220 us -> 212 us
    pallas_call x1, Pallas kernels: 208 us -> 200 us  [branch(): pl.pallas_call(functools.partial(move_kernel, unit), out_shape=(pltpu.VME...]
where the time goes in v15:
time: 215 us
  Pallas kernels  212 us (99%)
    pallas_call x1, Pallas kernels, branch(): pl.pallas_call(functools.partial(move_kernel, unit), out_shape=(pltpu.VME...  200 us
    pallas_call x1, Pallas kernels, branch(): pl.pallas_call(functools.partial(place_kernel, unit), out_shape=(jax.Shap...  12.2 us

profile of v15, /device:TPU:0, one launch (start us, length us, event | category | flops | bytes accessed | tf_op | source)
XLA Modules:
  0.0 214.8 jit_solution(3203972763523170370)
XLA Ops:
  1.3 213.4 %conditional.1 = ((bf16[2,3,2048,1024]{3,2,1,0:T(8,128)(2,1)}, bf16[2,3,512,2048]{3,2,1,0:T(8,128)(2,1)})) conditional(s32[]{:T(128)} %bitcast, (bf16[1,1,2048,1024]{3,2,1,0:T(8,128)(2,1)}, bf16[1,1,2048,1024]{3,2,1,0:T(8,128)(2,1)}, bf16[1,1,1024,2048]{3,2,1,0:T(8,128)(2,1)}, s32[16,2]{0,1:T(2,128)}) %tuple.55, ...), branch_computations={%region_0.0_spmd, %region_1.0_spmd, %region_2.0_spmd, %region_3.0_... | conditional | bytes 264 | solution.py:322
  1.5 0.8 copy.54.slot_map
  2.3 200.2 %move15.1 = (bf16[2,2048,1024]{2,1,0:T(8,128)(2,1)S(1)}, bf16[2,512,2048]{2,1,0:T(8,128)(2,1)S(1)}, bf16[2,2,2048,512]{3,2,1,0:T(8,128)(2,1)S(1)}, bf16[2,512,2048]{2,1,0:T(8,128)(2,1)S(1)}) custom-call(bf16[1,1,2048,1024]{3,2,1,0:T(8,128)(2,1)} %get-tuple-element.249.gate, bf16[1,1,2048,1024]{3,2,1,0:T(8,128)(2,1)} %get-tuple-element.250.up, ...), custom_call_target="tpu_custom_call" | custom-call | tf_op jit(solution)/shard_map/cond/branch_15_fun/move15/pallas_call | solution.py:285
  202.5 12.2 %place.31 = (bf16[2,3,2048,1024]{3,2,1,0:T(8,128)(2,1)}, bf16[2,3,512,2048]{3,2,1,0:T(8,128)(2,1)}) custom-call(s32[16,2]{1,0:T(8,128)S(1)} %copy.54.slot_map, bf16[2,2048,1024]{2,1,0:T(8,128)(2,1)S(1)} %get-tuple-element.252.home13, bf16[2,512,2048]{2,1,0:T(8,128)(2,1)S(1)} %get-tuple-element.253.homed, ...), custom_call_target="tpu_custom_call" | custom-call | tf_op jit(solution)/shard_map/cond/branch_15_fun/place/pallas_call | solution.py:309

commit v16 on v15

--- a/solution.py
+++ b/solution.py
@@ -256,7 +256,7 @@
     fetch.wait()
     for layer in range(2):
         for t in range(2):
-            filled = slots[me, t] >= 0
+            filled = slots[t, me] >= 0
 
             @pl.when(filled)
             def _():
@@ -314,10 +314,10 @@
                 ),
                 in_specs=[pl.BlockSpec(memory_space=pltpu.HBM)] + [VMEM] * 4,
                 out_specs=(ANY, ANY),
-                scratch_shapes=[pltpu.SMEM((16, 2), jnp.int32), pltpu.VMEM((512, 1024), BF16), DMA, DMA],
+                scratch_shapes=[pltpu.SMEM((2, 16), jnp.int32), pltpu.VMEM((512, 1024), BF16), DMA, DMA],
                 compiler_params=pltpu.CompilerParams(vmem_limit_bytes=4 << 20),
                 name="place",
-            )(slot_map, *moved)
+            )(slot_map.T, *moved)
 
         return lax.switch(hot_units[0], [functools.partial(branch, u) for u in range(16)], gate, up, down, slot_map)
 

time: 215 us -> 213 us (level)
  no operation moved by 1% of the time
where the time goes in v16:
time: 213 us
  Pallas kernels  212 us (100%)
    pallas_call x1, Pallas kernels, branch(): pl.pallas_call(functools.partial(move_kernel, unit), out_shape=(pltpu.VME...  199 us
    pallas_call x1, Pallas kernels, branch(): pl.pallas_call(functools.partial(place_kernel, unit), out_shape=(jax.Shap...  12.2 us

profile of v16, /device:TPU:0, one launch (start us, length us, event | category | flops | bytes accessed | tf_op | source)
XLA Modules:
  0.0 213.3 jit_solution(11908014456263675261)
XLA Ops:
  1.3 211.8 %conditional.1 = ((bf16[2,3,2048,1024]{3,2,1,0:T(8,128)(2,1)}, bf16[2,3,512,2048]{3,2,1,0:T(8,128)(2,1)})) conditional(s32[]{:T(128)} %bitcast.16, (s32[16,2]{0,1:T(2,128)}, bf16[1,1,2048,1024]{3,2,1,0:T(8,128)(2,1)}, bf16[1,1,2048,1024]{3,2,1,0:T(8,128)(2,1)}, bf16[1,1,1024,2048]{3,2,1,0:T(8,128)(2,1)}) %tuple.55, ...), branch_computations={%region_0.0_spmd, %region_1.0_spmd, %region_2.0_spmd, %region_3.0_... | conditional | bytes 548 | solution.py:322
  1.5 0.0 copy-start.8
  1.5 199.4 %move8.1 = (bf16[2,2048,1024]{2,1,0:T(8,128)(2,1)S(1)}, bf16[2,512,2048]{2,1,0:T(8,128)(2,1)S(1)}, bf16[2,2,2048,512]{3,2,1,0:T(8,128)(2,1)S(1)}, bf16[2,512,2048]{2,1,0:T(8,128)(2,1)S(1)}) custom-call(bf16[1,1,2048,1024]{3,2,1,0:T(8,128)(2,1)} %get-tuple-element.193.gate, bf16[1,1,2048,1024]{3,2,1,0:T(8,128)(2,1)} %get-tuple-element.194.up, ...), custom_call_target="tpu_custom_call" | custom-call | tf_op jit(solution)/shard_map/cond/branch_8_fun/move8/pallas_call | solution.py:285
  200.9 0.0 copy-done.8
  200.9 12.2 %place.24 = (bf16[2,3,2048,1024]{3,2,1,0:T(8,128)(2,1)}, bf16[2,3,512,2048]{3,2,1,0:T(8,128)(2,1)}) custom-call(s32[2,16]{1,0:T(2,128)S(1)} %bitcast.25, bf16[2,2048,1024]{2,1,0:T(8,128)(2,1)S(1)} %get-tuple-element.196.home13, bf16[2,512,2048]{2,1,0:T(8,128)(2,1)S(1)} %get-tuple-element.197.homed, bf16[2,2,2048,512]{3,2,1,0:T(8,128)(2,1)S(1)} %get-tuple-element.198.hot13, ...), custom_call_target="tpu_custom_call" | custom-call | tf_op jit(solution)/shard_map/cond/branch_8_fun/place/pallas_call | solution.py:309
Async XLA Ops:
  1.5 199.4 %copy-start.8 = (s32[16,2]{0,1:T(2,128)S(1)}, s32[16,2]{0,1:T(2,128)}, u32[]{:S(2)}) copy-start(s32[16,2]{0,1:T(2,128)} %get-tuple-element.192) | copy-start | bytes 388 | tf_op jit(solution)/shard_map/cond

commit v17 on v16

--- a/solution.py
+++ b/solution.py
@@ -24,7 +24,7 @@
 CHILDREN = tuple(tuple(tuple(v for v in range(1, 8) if par[v] == r) for r in range(8)) for par in PARENT)
 DEEPEST = max(map(max, DEPTH))
 N = 32
-HOME_AT = 3
+HOME_AT = 1
 LAG = 4
 
 

time: 213 us -> 211 us (level)
  Pallas kernels: 212 us -> 208 us
    pallas_call x1, Pallas kernels: 199 us -> 196 us  [branch(): pl.pallas_call(functools.partial(move_kernel, unit), out_shape=(pltpu.VME...]
where the time goes in v17:
time: 211 us; the launch traced here: 210 us
  Pallas kernels  208 us (99%)
    pallas_call x1, Pallas kernels, branch(): pl.pallas_call(functools.partial(move_kernel, unit), out_shape=(pltpu.VME...  196 us
    pallas_call x1, Pallas kernels, branch(): pl.pallas_call(functools.partial(place_kernel, unit), out_shape=(jax.Shap...  12.2 us

profile of v17, /device:TPU:0, one launch (start us, length us, event | category | flops | bytes accessed | tf_op | source)
XLA Modules:
  0.0 209.9 jit_solution(14542594737234996418)
XLA Ops:
  1.3 208.5 %conditional.1 = ((bf16[2,3,2048,1024]{3,2,1,0:T(8,128)(2,1)}, bf16[2,3,512,2048]{3,2,1,0:T(8,128)(2,1)})) conditional(s32[]{:T(128)} %bitcast.16, (s32[16,2]{0,1:T(2,128)}, bf16[1,1,2048,1024]{3,2,1,0:T(8,128)(2,1)}, bf16[1,1,2048,1024]{3,2,1,0:T(8,128)(2,1)}, bf16[1,1,1024,2048]{3,2,1,0:T(8,128)(2,1)}) %tuple.55, ...), branch_computations={%region_0.0_spmd, %region_1.0_spmd, %region_2.0_spmd, %region_3.0_... | conditional | bytes 548 | solution.py:322
  1.5 0.0 copy-start.8
  1.5 196.1 %move8.1 = (bf16[2,2048,1024]{2,1,0:T(8,128)(2,1)S(1)}, bf16[2,512,2048]{2,1,0:T(8,128)(2,1)S(1)}, bf16[2,2,2048,512]{3,2,1,0:T(8,128)(2,1)S(1)}, bf16[2,512,2048]{2,1,0:T(8,128)(2,1)S(1)}) custom-call(bf16[1,1,2048,1024]{3,2,1,0:T(8,128)(2,1)} %get-tuple-element.193.gate, bf16[1,1,2048,1024]{3,2,1,0:T(8,128)(2,1)} %get-tuple-element.194.up, ...), custom_call_target="tpu_custom_call" | custom-call | tf_op jit(solution)/shard_map/cond/branch_8_fun/move8/pallas_call | solution.py:285
  197.6 0.0 copy-done.8
  197.6 12.2 %place.24 = (bf16[2,3,2048,1024]{3,2,1,0:T(8,128)(2,1)}, bf16[2,3,512,2048]{3,2,1,0:T(8,128)(2,1)}) custom-call(s32[2,16]{1,0:T(2,128)S(1)} %bitcast.25, bf16[2,2048,1024]{2,1,0:T(8,128)(2,1)S(1)} %get-tuple-element.196.home13, bf16[2,512,2048]{2,1,0:T(8,128)(2,1)S(1)} %get-tuple-element.197.homed, bf16[2,2,2048,512]{3,2,1,0:T(8,128)(2,1)S(1)} %get-tuple-element.198.hot13, ...), custom_call_target="tpu_custom_call" | custom-call | tf_op jit(solution)/shard_map/cond/branch_8_fun/place/pallas_call | solution.py:309
Async XLA Ops:
  1.5 196.1 %copy-start.8 = (s32[16,2]{0,1:T(2,128)S(1)}, s32[16,2]{0,1:T(2,128)}, u32[]{:S(2)}) copy-start(s32[16,2]{0,1:T(2,128)} %get-tuple-element.192) | copy-start | bytes 388 | tf_op jit(solution)/shard_map/cond
